TPU v7x, 32 devices: a whole 2x2x4 slice. The times are simulated.
32 devices in a mesh: gx: 8 (over z, y), gy: 4 (over x, core).
Axes of the slice: x: 2, y: 2, z: 4, core: 2. Of those that a mesh axis runs over, the one named last changes fastest.
Arguments:
- snapshots: bfloat16 [8, 8, 4, 2048, 512], P('gx', 'gy'), may hold values from -120 to 120
- basis: bfloat16 [8, 8, 4, 24, 2048], P('gx', 'gy'), may hold values from -0.0625 to 0.0625
- node_counts: int32 [8, 8], P('gx', 'gy'), may hold values from 1024 to 2048, as said below
- adjacency: int32 [8, 8, 3], P('gx', 'gy'), may hold values from 0 to 63, as said below
Outputs:
- operator: float32 [8, 8, 397, 24], P('gx', 'gy')
- reduced_states: float32 [8, 8, 24, 512], P('gx', 'gy')
Inputs may be any that keep to these rules, and one draw needn't show every extreme that they name: Node slot n of subdomain g is live iff n < node_counts[g]; at least 1024 slots are live, and one subdomain has all 2048 live. Subdomain (row, col) has id row * 8 + col. Each row of adjacency holds 3 distinct ids other than its own subdomain's, each within one subdomain row and one subdomain column of it.
All inputs are finite; a program needn't handle non-finite values.
Results may differ from a plain program's by a relative error of at most 0.0003.
Values sent between devices are 32-bit elements; how exact they have to be, the bound alone decides.
A program may use at most 64 MiB of HBM per device.

v0:
```python
import jax
import jax.numpy as jnp
from jax import lax
from jax.experimental import pallas as pl
from jax.experimental.pallas import tpu as pltpu
from jax.sharding import PartitionSpec as P

beta_linear = 0.5
beta_quad = 0.5
LANES = 128
SUB = 8
HIGH = lax.Precision.HIGHEST


def spread_row(tile, row):
    return jnp.broadcast_to(tile[row : row + 1, :], tile.shape)


def spread_lane(tile, lane):
    if isinstance(lane, int):
        return jnp.broadcast_to(tile[:, lane : lane + 1], tile.shape)
    return jnp.take_along_axis(tile, jnp.full(tile.shape, lane, jnp.int32), axis=1)


def reduce_panel(tiles, base):
    sub = lax.broadcasted_iota(jnp.int32, (SUB, LANES), 0)
    lane = lax.broadcasted_iota(jnp.int32, (SUB, LANES), 1)
    inside = (lane >= base) & (lane < base + SUB)
    unit = (lane - base == sub).astype(jnp.float32)
    count = len(tiles)
    cols = [[spread_lane(t, base + j) for j in range(SUB)] for t in tiles]
    tiles = [jnp.where(inside, unit, t) for t in tiles]
    for j in range(SUB):
        for s in range(count):
            here = cols[s][j]
            inv = 1.0 / spread_row(here, j)
            row = spread_row(tiles[s], j) * inv
            tiles[s] = jnp.where(sub == j, row, tiles[s] - here * row)
            for i in range(j + 1, SUB):
                row = spread_row(cols[s][i], j) * inv
                cols[s][i] = jnp.where(sub == j, row, cols[s][i] - here * row)
    return tiles, inside


def clear_rows(tile, base, inside, rows):
    out = jnp.where(inside, 0.0, tile)
    terms = [spread_lane(tile, base + j) * rows[j] for j in range(SUB)]
    while len(terms) > 1:
        terms = [a + b for a, b in zip(terms[::2], terms[1::2])]
    return out - terms[0]


def mm(a, b):
    return jnp.dot(a, b, precision=HIGH, preferred_element_type=jnp.float32)


def mm_t(a, b):
    return lax.dot_general(
        a, b, (((1,), (1,)), ((), ())), precision=HIGH, preferred_element_type=jnp.float32
    )


def fit_kernel(nlin, gnorm_ref, state_ref, near_ref, out_ref, kept_ref, f_ref, tail_ref, m_ref, d_ref):
    subs, ranks, steps = state_ref.shape
    nf = out_ref.shape[1]
    pad = f_ref.shape[1]
    blocks = nf // LANES
    head = blocks * LANES
    rest = pad - head
    gnorm = gnorm_ref[0:1, 0:1]
    kept_ref[...] = state_ref[...]
    keep = (lax.broadcasted_iota(jnp.int32, (1, steps), 1) < steps - 1).astype(jnp.float32)
    for s in range(subs):
        state = state_ref[s]
        past = state * keep
        f_ref[s, nf - nf % SUB : pad, :] = jnp.zeros((pad - nf + nf % SUB, steps), jnp.float32)
        f_ref[s, 0:1, :] = keep
        f_ref[s, 1 : 1 + ranks, :] = past
        f_ref[s, 1 + ranks : nlin, :] = near_ref[s] * keep
        at = nlin
        for first in range(ranks):
            f_ref[s, at : at + ranks - first, :] = past[first : first + 1] * state[first:]
            at += ranks - first
        tail_ref[s] = jnp.zeros(tail_ref.shape[1:], jnp.float32)
        tail_ref[s, 0:ranks, :] = pltpu.roll(state, steps - 1, 1)
        tail_ref[s, ranks : ranks + rest, :] = f_ref[s, head:pad, :]
    row = lax.broadcasted_iota(jnp.int32, (pad, head + LANES), 0)
    col = lax.broadcasted_iota(jnp.int32, (pad, head + LANES), 1)
    level = jnp.where(row < nlin, beta_linear * gnorm, beta_quad * gnorm * gnorm) * steps
    level = jnp.where(row < nf, level, 1.0)
    shift = jnp.where(row < head, 0, ranks)
    ridge = jnp.where(col == row + shift, level, 0.0)
    for s in range(subs):
        feats = f_ref[s]
        m_ref[s, :, 0:head] = mm_t(feats, f_ref[s, 0:head, :]) + ridge[:, 0:head]
        m_ref[s, :, head:] = mm_t(feats, tail_ref[s]) + ridge[:, head:]

    def block(k, carry):
        at = pl.multiple_of(k * LANES, LANES)
        for s in range(subs):
            d_ref[s] = m_ref[s, pl.ds(at, LANES), pl.ds(at, LANES)]

        def panel(p, carry):
            base = p * SUB
            here = pl.ds(pl.multiple_of(base, SUB), SUB)
            done, inside = reduce_panel([d_ref[s, here, :] for s in range(subs)], base)
            for s in range(subs):
                rows = [spread_row(done[s], j) for j in range(SUB)]
                for r in range(0, LANES, SUB):
                    d_ref[s, r : r + SUB, :] = clear_rows(d_ref[s, r : r + SUB, :], base, inside, rows)
                d_ref[s, here, :] = done[s]
            return carry

        lax.fori_loop(0, LANES // SUB, panel, 0)
        for s in range(subs):
            rows = mm(d_ref[s], m_ref[s, pl.ds(at, LANES), :])
            m_ref[s] = m_ref[s] - mm(m_ref[s, :, pl.ds(at, LANES)], rows)
            m_ref[s, pl.ds(at, LANES), :] = rows
        return carry

    lax.fori_loop(0, blocks, block, 0)
    groups = rest // SUB
    tiles = [[m_ref[s, head + SUB * g : head + SUB * g + SUB, head:] for g in range(groups)] for s in range(subs)]
    for p in range(groups):
        base = ranks + p * SUB
        done, inside = reduce_panel([tiles[s][p] for s in range(subs)], base)
        for s in range(subs):
            rows = [spread_row(done[s], j) for j in range(SUB)]
            tiles[s] = [done[s] if g == p else clear_rows(tiles[s][g], base, inside, rows) for g in range(groups)]
    for s in range(subs):
        last = jnp.concatenate(tiles[s], axis=0)
        known = m_ref[s, 0:head, head:]
        out_ref[s, 0:head, :] = (known - mm(known[:, ranks : ranks + rest], last))[:, 0:ranks]
        out_ref[s, head:nf, :] = last[0 : nf - head, 0:ranks]


def fit(gnorm, states, near):
    subs, ranks, steps = states.shape
    nlin = 1 + ranks + near.shape[1]
    nf = nlin + ranks * (ranks + 1) // 2
    pad = -(-nf // SUB) * SUB
    head = nf // LANES * LANES

    def kernel(*refs):
        fit_kernel(nlin, *refs)

    vmem = pl.BlockSpec(memory_space=pltpu.VMEM)
    return pl.pallas_call(
        kernel,
        out_shape=(
            jax.ShapeDtypeStruct((subs, nf, ranks), jnp.float32),
            jax.ShapeDtypeStruct(states.shape, jnp.float32),
        ),
        in_specs=[vmem, vmem, vmem],
        out_specs=(vmem, vmem),
        scratch_shapes=[
            pltpu.VMEM((subs, pad, steps), jnp.float32),
            pltpu.VMEM((subs, LANES, steps), jnp.float32),
            pltpu.VMEM((subs, pad, head + LANES), jnp.float32),
            pltpu.VMEM((subs, LANES, LANES), jnp.float32),
        ],
        compiler_params=pltpu.CompilerParams(vmem_limit_bytes=40 * 2**20),
        name="fit",
    )(gnorm, states, near)


def share_kernel(sizes, counts_ref, links_ref, proj_ref, slotsq_ref, near_ref, state_ref, gnorm_ref,
                 stat_ref, half_ref, row_ref, col_ref, cell_ref, row_sems, col_sems, halo_sems):
    nx, ny = sizes
    subs, nvar, ranks, steps = proj_ref.shape
    slots = slotsq_ref.shape[2]
    nbrs = links_ref.shape[1]
    x, y = lax.axis_index("gx"), lax.axis_index("gy")
    barrier = pltpu.get_barrier_semaphore()
    sides = [(dx, dy) for dx in (-1, 0, 1) for dy in (-1, 0, 1) if dx or dy]

    def at(dx, dy):
        return (lax.rem(x + dx + nx, nx), lax.rem(y + dy + ny, ny))

    greeted = [at(d, 0) for d in range(1, nx)] + [at(0, d) for d in range(1, ny)]
    greeted += [at(dx, dy) for dx, dy in sides if dx and dy]
    for other in greeted:
        pl.semaphore_signal(barrier, inc=1, device_id=other, device_id_type=pl.DeviceIdType.MESH)

    pairs = [(v, w) for v in range(nvar) for w in range(v, nvar)]
    lane = lax.broadcasted_iota(jnp.int32, (1, LANES), 1)
    stat_ref[...] = jnp.zeros(stat_ref.shape, jnp.float32)
    squares = jnp.zeros((nvar, LANES), jnp.float32)
    nodes = 0
    for s in range(subs):
        nodes = nodes + counts_ref[s]
        for p in range(0, slots, LANES):
            squares += jnp.where(lane + p < counts_ref[s], slotsq_ref[s, :, p : p + LANES], 0.0)
    stat_ref[0:nvar, :] = squares
    for i, (v, w) in enumerate(pairs):
        total = jnp.zeros((ranks, LANES), jnp.float32)
        for s in range(subs):
            for k in range(0, steps, LANES):
                total += proj_ref[s, v, :, k : k + LANES] * proj_ref[s, w, :, k : k + LANES]
        stat_ref[nvar + i : nvar + i + 1, :] = jnp.sum(total, axis=0, keepdims=True)
    last = nvar + len(pairs)
    stat_ref[last : last + 1, :] = jnp.where(lane == 0, nodes.astype(jnp.float32), 0.0)

    pl.semaphore_wait(barrier, len(greeted))

    def gather(src, slots_ref, sems, me, count, step):
        slots_ref[me] = src[...]
        copies = []
        for d in range(1, count):
            copies.append(
                pltpu.make_async_remote_copy(
                    src_ref=src,
                    dst_ref=slots_ref.at[me],
                    send_sem=sems.at[0, d],
                    recv_sem=sems.at[1, d],
                    device_id=step(d),
                    device_id_type=pl.DeviceIdType.MESH,
                )
            )
            copies[-1].start()
        for copy in copies:
            copy.wait_recv()
        total = slots_ref[0]
        for d in range(1, count):
            total = total + slots_ref[d]
        return total, copies

    half, sent = gather(stat_ref, row_ref, row_sems, x, nx, lambda d: at(d, 0))
    half_ref[...] = half
    total, more = gather(half_ref, col_ref, col_sems, y, ny, lambda d: at(0, d))
    sent += more
    total = jnp.broadcast_to(jnp.sum(total, axis=1, keepdims=True), total.shape)
    nodes = total[last : last + 1, :]
    scale = [jnp.sqrt(total[v : v + 1, :] / (nodes * steps) + 1e-06) for v in range(nvar)]
    gnorm = jnp.zeros((1, LANES), jnp.float32)
    for i, (v, w) in enumerate(pairs):
        gnorm += (1.0 if v == w else 2.0) * total[nvar + i : nvar + i + 1, :] / (scale[v] * scale[w])
    gnorm = gnorm / (nx * ny * subs * ranks * steps)
    gnorm_ref[...] = jnp.broadcast_to(gnorm, gnorm_ref.shape)
    inverse = [1.0 / part[:, 0:1] for part in scale]
    wide = subs + 2
    for s in range(subs):
        state = proj_ref[s, 0] * inverse[0]
        for v in range(1, nvar):
            state = state + proj_ref[s, v] * inverse[v]
        state_ref[s] = state
        cell_ref[wide + 1 + s] = state
    for i, (dx, dy) in enumerate(sides):
        first, size = (0, subs) if dy == 0 else ((subs - 1, 1) if dy > 0 else (0, 1))
        into = (1 - dx) * wide + (1 if dy == 0 else (0 if dy > 0 else subs + 1))
        copy = pltpu.make_async_remote_copy(
            src_ref=cell_ref.at[pl.ds(wide + 1 + first, size)],
            dst_ref=cell_ref.at[pl.ds(into, size)],
            send_sem=halo_sems.at[0, i],
            recv_sem=halo_sems.at[1, i],
            device_id=at(dx, dy),
            device_id_type=pl.DeviceIdType.MESH,
        )
        copy.start()
        sent.append(copy)
    for i, (dx, dy) in enumerate(sides):
        sent[len(sent) - len(sides) + i].wait_recv()
    for copy in sent:
        copy.wait_send()
    columns = ny * subs
    for s in range(subs):
        for b in range(nbrs):
            link = links_ref[s, b]
            row = link // columns
            cell = (row - x + 1) * wide + link - row * columns - y * subs + 1
            cell = jnp.clip(cell, 0, 3 * wide - 1)
            near_ref[s, b * ranks : b * ranks + ranks, :] = cell_ref[cell]


def share(counts, links, proj, slotsq):
    nx, ny = lax.axis_size("gx"), lax.axis_size("gy")
    subs, nvar, ranks, steps = proj.shape
    rows = -(-(nvar + nvar * (nvar + 1) // 2 + 1) // SUB) * SUB
    smem = pl.BlockSpec(memory_space=pltpu.SMEM)
    vmem = pl.BlockSpec(memory_space=pltpu.VMEM)

    def kernel(*refs):
        share_kernel((nx, ny), *refs)

    return pl.pallas_call(
        kernel,
        out_shape=(
            jax.ShapeDtypeStruct((subs, links.shape[1] * ranks, steps), jnp.float32),
            jax.ShapeDtypeStruct((subs, ranks, steps), jnp.float32),
            jax.ShapeDtypeStruct((SUB, LANES), jnp.float32),
        ),
        in_specs=[smem, smem, vmem, vmem],
        out_specs=(vmem, vmem, vmem),
        scratch_shapes=[
            pltpu.VMEM((rows, LANES), jnp.float32),
            pltpu.VMEM((rows, LANES), jnp.float32),
            pltpu.VMEM((nx, rows, LANES), jnp.float32),
            pltpu.VMEM((ny, rows, LANES), jnp.float32),
            pltpu.VMEM((3 * (subs + 2), ranks, steps), jnp.float32),
            pltpu.SemaphoreType.DMA((2, nx)),
            pltpu.SemaphoreType.DMA((2, ny)),
            pltpu.SemaphoreType.DMA((2, 8)),
        ],
        compiler_params=pltpu.CompilerParams(collective_id=0, has_side_effects=True),
        name="share",
    )(counts, links, proj, slotsq)


def body(snapshots, basis, node_counts, adjacency):
    values = snapshots[0]
    modes = basis[0]
    counts = node_counts[0]
    slots = values.shape[2]
    live = jnp.arange(slots, dtype=jnp.int32)[None, :] < counts[:, None]
    masked = modes * live.astype(jnp.bfloat16)[:, None, None, :]
    proj = jnp.einsum("svrp,svpk->svrk", masked, values, preferred_element_type=jnp.float32)
    slotsq = jnp.einsum("svpk,svpk->svp", values, values, preferred_element_type=jnp.float32)
    near, states, gnorm = share(counts, adjacency[0], proj, slotsq)
    operator, states = fit(gnorm, states, near)
    return (operator[None], states[None])


def solution(mesh):
    in_specs = (
        P("gx", "gy", None, None, None),
        P("gx", "gy", None, None, None),
        P("gx", "gy"),
        P("gx", "gy", None),
    )
    out_specs = (P("gx", "gy", None, None), P("gx", "gy", None, None))
    return jax.shard_map(body, mesh=mesh, in_specs=in_specs, out_specs=out_specs, check_vma=False)
```

profile of v0, /device:TPU:0, one launch (start us, length us, event | category | flops | bytes accessed | tf_op | source)
XLA Modules:
  0.0 98.8 jit_solution(1108270169830005885)
XLA Ops:
  0.6 0.0 copy-start.3
  0.6 0.9 compare_convert_fusion
  1.5 8.2 %fusion.refs_3_ = f32[2,4,2048]{2,1,0:T(4,128)} fusion(bf16[1,2,4,2048,512]{4,3,2,1,0:T(8,128)(2,1)} %param.4), kind=kLoop, calls=%fused_computation.1 | loop fusion | flops 25149440 | bytes 16842752 | tf_op jit(solution)/shard_map/svpk,svpk->svp/dot_general | solution.py:317
  9.7 1.6 %copy-done.3 = bf16[1,2,4,2048,512]{4,3,2,1,0:T(8,128)(2,1)S(1)} copy-done((bf16[1,2,4,2048,512]{4,3,2,1,0:T(8,128)(2,1)S(1)}, bf16[1,2,4,2048,512]{4,3,2,1,0:T(8,128)(2,1)}, u32[]{:S(2)}) %copy-start.3) | copy-done | bytes 16777240
  11.3 4.2 %fusion.1.refs_2_ = f32[2,4,24,512]{3,2,1,0:T(8,128)} fusion(bf16[1,2,4,2048,512]{4,3,2,1,0:T(8,128)(2,1)S(1)} %copy-done.3, bf16[1,2,4,24,2048]{4,3,2,1,0:T(8,128)(2,1)} %param.5, bf16[2,2048]{1,0:T(2,128)(2,1)S(1)} %compare_convert_fusion), kind=kOutput, calls=%fused_computation.2 | convolution fusion | flops 403046400 | bytes 17965056 | tf_op jit(solution)/shard_map/svrp,svpk->svrk/dot_general | solution.py:316
  15.5 24.3 %share.1 = (f32[2,72,512]{2,1,0:T(8,128)}, f32[2,24,512]{2,1,0:T(8,128)}, f32[8,128]{1,0:T(8,128)}) custom-call(s32[2]{0:T(128)} %bitcast.13, s32[2,3]{1,0:T(2,128)} %bitcast.14, f32[2,4,24,512]{3,2,1,0:T(8,128)} %fusion.1.refs_2_, f32[2,4,2048]{2,1,0:T(4,128)} %fusion.refs_3_), custom_call_target="tpu_custom_call" | custom-call | tf_op jit(solution)/shard_map/share/pallas_call | solution.py:285
  39.8 0.0 copy-start
  39.8 1.0 copy-done
  40.7 0.0 copy-start.1
  40.7 0.9 copy-done.1
  41.6 0.0 copy-start.2
  41.6 0.7 copy-done.2
  42.3 55.7 %fit.1 = (f32[2,397,24]{2,1,0:T(8,128)S(1)}, f32[2,24,512]{2,1,0:T(8,128)}) custom-call(f32[8,128]{1,0:T(8,128)S(1)} %copy-done.2, f32[2,24,512]{2,1,0:T(8,128)S(1)} %copy-done.1, f32[2,72,512]{2,1,0:T(8,128)S(1)} %copy-done), custom_call_target="tpu_custom_call" | custom-call | tf_op jit(solution)/shard_map/fit/pallas_call | solution.py:148
  98.0 0.8 copy.6
Async XLA Ops:
  0.6 10.7 %copy-start.3 = (bf16[1,2,4,2048,512]{4,3,2,1,0:T(8,128)(2,1)S(1)}, bf16[1,2,4,2048,512]{4,3,2,1,0:T(8,128)(2,1)}, u32[]{:S(2)}) copy-start(bf16[1,2,4,2048,512]{4,3,2,1,0:T(8,128)(2,1)} %param.4) | copy-start | bytes 50331652
  39.8 1.0 copy-start
  40.7 0.9 copy-start.1
  41.6 0.7 copy-start.2
where the time goes:
time: 99.2 us; the launch traced here: 98.8 us
  Pallas kernels  79.9 us (81%)
  other arithmetic  9.09 us (9%)
  local copies, waits for them, and re-layouts  4.93 us (5%)
  matrix products  4.18 us (4%)
    pallas_call x1, Pallas kernels, fit(): pl.pallas_call(kernel, out_shape=(jax.ShapeDtypeStruct((subs, nf, ranks),...  55.7 us
    pallas_call x1, Pallas kernels, share(): pl.pallas_call(kernel, out_shape=(jax.ShapeDtypeStruct((subs, links.shape...  24.3 us
    dot_general x1, other arithmetic, body(): jnp.einsum('svpk,svpk->svp', values, values, preferred_element_type=jnp.f...  8.21 us
    unnamed x9, local copies, waits for them, and re-layouts  4.93 us
    dot_general x1, matrix products, body(): jnp.einsum('svrp,svpk->svrk', masked, values, preferred_element_type=jnp....  4.18 us

commit v1 on v0

--- a/solution.py
+++ b/solution.py
@@ -9,7 +9,6 @@
 beta_quad = 0.5
 LANES = 128
 SUB = 8
-HIGH = lax.Precision.HIGHEST
 
 
 def spread_row(tile, row):
@@ -17,147 +16,204 @@
 
 
 def spread_lane(tile, lane):
-    if isinstance(lane, int):
-        return jnp.broadcast_to(tile[:, lane : lane + 1], tile.shape)
-    return jnp.take_along_axis(tile, jnp.full(tile.shape, lane, jnp.int32), axis=1)
-
-
-def reduce_panel(tiles, base):
+    return jnp.broadcast_to(tile[:, lane : lane + 1], tile.shape)
+
+
+def split3(a):
+    hi = a.astype(jnp.bfloat16)
+    left = a - hi.astype(jnp.float32)
+    mid = left.astype(jnp.bfloat16)
+    low = (left - mid.astype(jnp.float32)).astype(jnp.bfloat16)
+    return hi, mid, low
+
+
+def as_left(parts):
+    hi, mid, low = parts
+    return jnp.concatenate([hi, mid, hi, mid, hi, low], axis=1)
+
+
+def as_right(parts, axis=1):
+    hi, mid, low = parts
+    return jnp.concatenate([hi, mid, mid, hi, low, hi], axis=axis)
+
+
+def dot_nt(a, b):
+    return lax.dot_general(a, b, (((1,), (1,)), ((), ())), preferred_element_type=jnp.float32)
+
+
+def dot_nn(a, b):
+    return jnp.dot(a, b, preferred_element_type=jnp.float32)
+
+
+def whiten(blocks):
+    size = blocks[0].shape[0]
     sub = lax.broadcasted_iota(jnp.int32, (SUB, LANES), 0)
     lane = lax.broadcasted_iota(jnp.int32, (SUB, LANES), 1)
-    inside = (lane >= base) & (lane < base + SUB)
-    unit = (lane - base == sub).astype(jnp.float32)
-    count = len(tiles)
-    cols = [[spread_lane(t, base + j) for j in range(SUB)] for t in tiles]
-    tiles = [jnp.where(inside, unit, t) for t in tiles]
-    for j in range(SUB):
+    count = len(blocks)
+    tiles = [[b[r : r + SUB, :] for r in range(0, size, SUB)] for b in blocks]
+    out = [[] for b in blocks]
+    for p in range(size // SUB):
+        base = p * SUB
+        inside = (lane >= base) & (lane < base + SUB)
+        unit = (lane - base == sub).astype(jnp.float32)
+        cols = [[spread_lane(t[p], base + j) for j in range(SUB)] for t in tiles]
+        here = [jnp.where(inside, unit, t[p]) for t in tiles]
+        scaled = [jnp.zeros((SUB, LANES), jnp.float32) for t in tiles]
+        for j in range(SUB):
+            for s in range(count):
+                col = cols[s][j]
+                pivot = spread_row(col, j)
+                inv = 1.0 / pivot
+                row = spread_row(here[s], j)
+                scaled[s] = jnp.where(sub == j, row * lax.rsqrt(pivot), scaled[s])
+                row = row * inv
+                here[s] = jnp.where(sub == j, row, here[s] - col * row)
+                for i in range(j + 1, SUB):
+                    row = spread_row(cols[s][i], j) * inv
+                    cols[s][i] = jnp.where(sub == j, row, cols[s][i] - col * row)
         for s in range(count):
-            here = cols[s][j]
-            inv = 1.0 / spread_row(here, j)
-            row = spread_row(tiles[s], j) * inv
-            tiles[s] = jnp.where(sub == j, row, tiles[s] - here * row)
-            for i in range(j + 1, SUB):
-                row = spread_row(cols[s][i], j) * inv
-                cols[s][i] = jnp.where(sub == j, row, cols[s][i] - here * row)
-    return tiles, inside
-
-
-def clear_rows(tile, base, inside, rows):
-    out = jnp.where(inside, 0.0, tile)
-    terms = [spread_lane(tile, base + j) * rows[j] for j in range(SUB)]
-    while len(terms) > 1:
-        terms = [a + b for a, b in zip(terms[::2], terms[1::2])]
-    return out - terms[0]
-
-
-def mm(a, b):
-    return jnp.dot(a, b, precision=HIGH, preferred_element_type=jnp.float32)
-
-
-def mm_t(a, b):
-    return lax.dot_general(
-        a, b, (((1,), (1,)), ((), ())), precision=HIGH, preferred_element_type=jnp.float32
-    )
-
-
-def fit_kernel(nlin, gnorm_ref, state_ref, near_ref, out_ref, kept_ref, f_ref, tail_ref, m_ref, d_ref):
+            out[s].append(jnp.where(lane < base + SUB, scaled[s], 0.0))
+            rows = [spread_row(here[s], j) for j in range(SUB)]
+            for r in range(p + 1, size // SUB):
+                tile = tiles[s][r]
+                terms = [spread_lane(tile, base + j) * rows[j] for j in range(SUB)]
+                while len(terms) > 1:
+                    terms = [a + b for a, b in zip(terms[::2], terms[1::2])]
+                tiles[s][r] = jnp.where(inside, 0.0, tile) - terms[0]
+    return [jnp.concatenate(o, axis=0) for o in out]
+
+
+def fit_kernel(gnorm_ref, state_ref, near_ref, out_ref, kept_ref, f_ref, hi_ref, mid_ref, low_ref):
     subs, ranks, steps = state_ref.shape
-    nf = out_ref.shape[1]
-    pad = f_ref.shape[1]
+    near = near_ref.shape[1]
+    nquad = ranks * (ranks + 1) // 2
+    nself = ranks + nquad + 1
+    nf = nself + near
     blocks = nf // LANES
     head = blocks * LANES
-    rest = pad - head
+    rest = -(-(nf - head) // SUB) * SUB
+    tall = head + ranks + rest
     gnorm = gnorm_ref[0:1, 0:1]
     kept_ref[...] = state_ref[...]
     keep = (lax.broadcasted_iota(jnp.int32, (1, steps), 1) < steps - 1).astype(jnp.float32)
+    last = nf - head
     for s in range(subs):
         state = state_ref[s]
         past = state * keep
-        f_ref[s, nf - nf % SUB : pad, :] = jnp.zeros((pad - nf + nf % SUB, steps), jnp.float32)
-        f_ref[s, 0:1, :] = keep
-        f_ref[s, 1 : 1 + ranks, :] = past
-        f_ref[s, 1 + ranks : nlin, :] = near_ref[s] * keep
-        at = nlin
+        f_ref[s, 0:ranks, :] = past
+        at = ranks
         for first in range(ranks):
             f_ref[s, at : at + ranks - first, :] = past[first : first + 1] * state[first:]
             at += ranks - first
-        tail_ref[s] = jnp.zeros(tail_ref.shape[1:], jnp.float32)
-        tail_ref[s, 0:ranks, :] = pltpu.roll(state, steps - 1, 1)
-        tail_ref[s, ranks : ranks + rest, :] = f_ref[s, head:pad, :]
-    row = lax.broadcasted_iota(jnp.int32, (pad, head + LANES), 0)
-    col = lax.broadcasted_iota(jnp.int32, (pad, head + LANES), 1)
-    level = jnp.where(row < nlin, beta_linear * gnorm, beta_quad * gnorm * gnorm) * steps
-    level = jnp.where(row < nf, level, 1.0)
-    shift = jnp.where(row < head, 0, ranks)
-    ridge = jnp.where(col == row + shift, level, 0.0)
-    for s in range(subs):
-        feats = f_ref[s]
-        m_ref[s, :, 0:head] = mm_t(feats, f_ref[s, 0:head, :]) + ridge[:, 0:head]
-        m_ref[s, :, head:] = mm_t(feats, tail_ref[s]) + ridge[:, head:]
-
-    def block(k, carry):
-        at = pl.multiple_of(k * LANES, LANES)
+        f_ref[s, at : at + 1, :] = keep
+        there = near_ref[s] * keep
+        f_ref[s, nself:head, :] = there[0 : head - nself]
+        f_ref[s, head : head + ranks, :] = pltpu.roll(state, steps - 1, 1)
+        f_ref[s, tall - rest : tall, :] = jnp.zeros((rest, steps), jnp.float32)
+        f_ref[s, tall - rest : tall - rest + last, :] = there[head - nself :]
+        hi, mid, low = split3(f_ref[s])
+        hi_ref[s] = hi
+        mid_ref[s] = mid
+        low_ref[s] = low
+
+    def parts(s, first, size):
+        return [r[s, first : first + size, :] for r in (hi_ref, mid_ref, low_ref)]
+
+    linear = beta_linear * gnorm * steps
+    square = beta_quad * gnorm * gnorm * steps
+
+    def ridge(first, size, lanes):
+        row = lax.broadcasted_iota(jnp.int32, (size, lanes), 0)
+        col = lax.broadcasted_iota(jnp.int32, (size, lanes), 1)
+        at = row + first
+        level = jnp.where((at < ranks) | (at >= nself - 1), linear, square)
+        level = jnp.where(at < nf, level, 1.0)
+        return jnp.where(row == col, level, 0.0)
+
+    def gram(s, first, rows, at, lanes):
+        return dot_nt(as_left(parts(s, first, rows)), as_right(parts(s, at, lanes)))
+
+    g = []
+    for s in range(subs):
+        cols = []
+        for j in range(blocks):
+            at = j * LANES
+            top = gram(s, at, LANES, at, LANES) + ridge(at, LANES, LANES)
+            low = gram(s, at + LANES, tall - at - LANES, at, LANES)
+            cols.append([top, low])
+        right = gram(s, head, ranks, tall - rest, rest)
+        tip = gram(s, tall - rest, rest, tall - rest, rest) + ridge(head, rest, rest)
+        cols.append([tip, right])
+        g.append(cols)
+    roots = [[None] * (blocks + 1) for s in range(subs)]
+    sides = [[None] * blocks for s in range(subs)]
+    for k in range(blocks):
+        done = whiten([g[s][k][0] for s in range(subs)])
         for s in range(subs):
-            d_ref[s] = m_ref[s, pl.ds(at, LANES), pl.ds(at, LANES)]
-
-        def panel(p, carry):
-            base = p * SUB
-            here = pl.ds(pl.multiple_of(base, SUB), SUB)
-            done, inside = reduce_panel([d_ref[s, here, :] for s in range(subs)], base)
-            for s in range(subs):
-                rows = [spread_row(done[s], j) for j in range(SUB)]
-                for r in range(0, LANES, SUB):
-                    d_ref[s, r : r + SUB, :] = clear_rows(d_ref[s, r : r + SUB, :], base, inside, rows)
-                d_ref[s, here, :] = done[s]
-            return carry
-
-        lax.fori_loop(0, LANES // SUB, panel, 0)
-        for s in range(subs):
-            rows = mm(d_ref[s], m_ref[s, pl.ds(at, LANES), :])
-            m_ref[s] = m_ref[s] - mm(m_ref[s, :, pl.ds(at, LANES)], rows)
-            m_ref[s, pl.ds(at, LANES), :] = rows
-        return carry
-
-    lax.fori_loop(0, blocks, block, 0)
-    groups = rest // SUB
-    tiles = [[m_ref[s, head + SUB * g : head + SUB * g + SUB, head:] for g in range(groups)] for s in range(subs)]
-    for p in range(groups):
-        base = ranks + p * SUB
-        done, inside = reduce_panel([tiles[s][p] for s in range(subs)], base)
-        for s in range(subs):
-            rows = [spread_row(done[s], j) for j in range(SUB)]
-            tiles[s] = [done[s] if g == p else clear_rows(tiles[s][g], base, inside, rows) for g in range(groups)]
-    for s in range(subs):
-        last = jnp.concatenate(tiles[s], axis=0)
-        known = m_ref[s, 0:head, head:]
-        out_ref[s, 0:head, :] = (known - mm(known[:, ranks : ranks + rest], last))[:, 0:ranks]
-        out_ref[s, head:nf, :] = last[0 : nf - head, 0:ranks]
+            root = split3(done[s])
+            roots[s][k] = root
+            side = split3(dot_nt(as_left(split3(g[s][k][1])), as_right(root)))
+            sides[s][k] = side
+            left = as_left(side)
+            right = as_right(side)
+            rows = left.shape[0]
+            for j in range(k + 1, blocks):
+                at = (j - k - 1) * LANES
+                both = right[at : at + LANES]
+                g[s][j][0] = g[s][j][0] - dot_nt(left[at : at + LANES], both)
+                g[s][j][1] = g[s][j][1] - dot_nt(left[at + LANES :], both)
+            both = right[rows - rest :]
+            g[s][blocks][0] = g[s][blocks][0] - dot_nt(left[rows - rest :], both)
+            g[s][blocks][1] = g[s][blocks][1] - dot_nt(left[rows - rest - ranks : rows - rest], both)
+    tips = []
+    for s in range(subs):
+        tip = g[s][blocks][0]
+        tips.append(jnp.concatenate([tip, jnp.zeros((rest, LANES - rest), jnp.float32)], axis=1))
+    tips = whiten(tips)
+    for s in range(subs):
+        root = split3(tips[s])
+        wide = jnp.concatenate([g[s][blocks][1], jnp.zeros((ranks, LANES - rest), jnp.float32)], axis=1)
+        known = dot_nt(as_left(split3(wide)), as_right([jnp.concatenate([p, jnp.zeros((LANES - rest, LANES), p.dtype)], axis=0) for p in root]))
+        tail = dot_nn(as_left(split3(known)), as_right([jnp.concatenate([p, jnp.zeros((LANES - rest, LANES), p.dtype)], axis=0) for p in root], 0))
+        answer = [None] * (blocks + 1)
+        answer[blocks] = tail
+        for k in range(blocks - 1, -1, -1):
+            hi, mid, low = sides[s][k]
+            rows = hi.shape[0]
+            value = (hi.astype(jnp.float32) + mid.astype(jnp.float32)) + low.astype(jnp.float32)
+            total = value[rows - rest - ranks : rows - rest]
+            for j in range(k + 1, blocks):
+                at = (j - k - 1) * LANES
+                total = total - dot_nn(as_left(split3(answer[j])), as_right([p[at : at + LANES] for p in sides[s][k]], 0))
+            pads = [jnp.concatenate([p[rows - rest :], jnp.zeros((LANES - rest, LANES), p.dtype)], axis=0) for p in sides[s][k]]
+            total = total - dot_nn(as_left(split3(tail)), as_right(pads, 0))
+            answer[k] = dot_nn(as_left(split3(total)), as_right(roots[s][k], 0))
+        whole = jnp.concatenate(answer, axis=1)
+        out_ref[s] = jnp.concatenate(
+            [whole[:, nself - 1 : nself], whole[:, 0:ranks], whole[:, nself:nf], whole[:, ranks : nself - 1]], axis=1
+        )
 
 
 def fit(gnorm, states, near):
     subs, ranks, steps = states.shape
-    nlin = 1 + ranks + near.shape[1]
-    nf = nlin + ranks * (ranks + 1) // 2
-    pad = -(-nf // SUB) * SUB
+    nf = 1 + ranks + near.shape[1] + ranks * (ranks + 1) // 2
     head = nf // LANES * LANES
-
-    def kernel(*refs):
-        fit_kernel(nlin, *refs)
-
+    rest = -(-(nf - head) // SUB) * SUB
+    tall = head + ranks + rest
     vmem = pl.BlockSpec(memory_space=pltpu.VMEM)
     return pl.pallas_call(
-        kernel,
+        fit_kernel,
         out_shape=(
-            jax.ShapeDtypeStruct((subs, nf, ranks), jnp.float32),
+            jax.ShapeDtypeStruct((subs, ranks, nf), jnp.float32),
             jax.ShapeDtypeStruct(states.shape, jnp.float32),
         ),
         in_specs=[vmem, vmem, vmem],
         out_specs=(vmem, vmem),
         scratch_shapes=[
-            pltpu.VMEM((subs, pad, steps), jnp.float32),
-            pltpu.VMEM((subs, LANES, steps), jnp.float32),
-            pltpu.VMEM((subs, pad, head + LANES), jnp.float32),
-            pltpu.VMEM((subs, LANES, LANES), jnp.float32),
+            pltpu.VMEM((subs, tall, steps), jnp.float32),
+            pltpu.VMEM((subs, tall, steps), jnp.bfloat16),
+            pltpu.VMEM((subs, tall, steps), jnp.bfloat16),
+            pltpu.VMEM((subs, tall, steps), jnp.bfloat16),
         ],
         compiler_params=pltpu.CompilerParams(vmem_limit_bytes=40 * 2**20),
         name="fit",
@@ -317,7 +373,7 @@
     slotsq = jnp.einsum("svpk,svpk->svp", values, values, preferred_element_type=jnp.float32)
     near, states, gnorm = share(counts, adjacency[0], proj, slotsq)
     operator, states = fit(gnorm, states, near)
-    return (operator[None], states[None])
+    return (operator.swapaxes(1, 2)[None], states[None])
 
 
 def solution(mesh):

time: 99.2 us -> 64.7 us (0.65)
  Pallas kernels: 79.9 us -> 46.3 us
    pallas_call x1, Pallas kernels: 55.7 us -> 22.1 us  [fit(): pl.pallas_call(fit_kernel, out_shape=(jax.ShapeDtypeStruct((subs, ranks,...]
    unnamed x9 -> x8, local copies, waits for them, and re-layouts: 4.93 us -> 4.12 us
where the time goes in v1:
time: 64.7 us; the launch traced here: 64.4 us
  Pallas kernels  46.3 us (72%)
  other arithmetic  9.09 us (14%)
  matrix products  4.18 us (6%)
  local copies, waits for them, and re-layouts  4.12 us (6%)
  between operations  0.66 us (1%)
    pallas_call x1, Pallas kernels, share(): pl.pallas_call(kernel, out_shape=(jax.ShapeDtypeStruct((subs, links.shape...  24.3 us
    pallas_call x1, Pallas kernels, fit(): pl.pallas_call(fit_kernel, out_shape=(jax.ShapeDtypeStruct((subs, ranks,...  22.1 us
    dot_general x1, other arithmetic, body(): jnp.einsum('svpk,svpk->svp', values, values, preferred_element_type=jnp.f...  8.21 us
    dot_general x1, matrix products, body(): jnp.einsum('svrp,svpk->svrk', masked, values, preferred_element_type=jnp....  4.18 us
    unnamed x8, local copies, waits for them, and re-layouts  4.12 us

profile of v1, /device:TPU:0, one launch (start us, length us, event | category | flops | bytes accessed | tf_op | source)
XLA Modules:
  0.0 64.4 jit_solution(6563014248979638851)
XLA Ops:
  0.6 0.0 copy-start.3
  0.6 0.9 %compare_convert_fusion = bf16[2,2048]{1,0:T(2,128)(2,1)S(1)} fusion(s32[2]{0:T(128)} %bitcast.13), kind=kLoop, calls=%fused_computation.6 | loop fusion | flops 8192 | bytes 8200 | tf_op jit(solution)/shard_map/convert_element_type | solution.py:371
  1.5 8.2 %fusion.refs_3_ = f32[2,4,2048]{2,1,0:T(4,128)} fusion(bf16[1,2,4,2048,512]{4,3,2,1,0:T(8,128)(2,1)} %param.4), kind=kLoop, calls=%fused_computation.1 | loop fusion | flops 25149440 | bytes 16842752 | tf_op jit(solution)/shard_map/svpk,svpk->svp/dot_general | solution.py:373
  9.7 1.6 %copy-done.3 = bf16[1,2,4,2048,512]{4,3,2,1,0:T(8,128)(2,1)S(1)} copy-done((bf16[1,2,4,2048,512]{4,3,2,1,0:T(8,128)(2,1)S(1)}, bf16[1,2,4,2048,512]{4,3,2,1,0:T(8,128)(2,1)}, u32[]{:S(2)}) %copy-start.3) | copy-done | bytes 16777240
  11.3 4.2 %fusion.1.refs_2_ = f32[2,4,24,512]{3,2,1,0:T(8,128)} fusion(bf16[1,2,4,2048,512]{4,3,2,1,0:T(8,128)(2,1)S(1)} %copy-done.3, bf16[1,2,4,24,2048]{4,3,2,1,0:T(8,128)(2,1)} %param.5, bf16[2,2048]{1,0:T(2,128)(2,1)S(1)} %compare_convert_fusion), kind=kOutput, calls=%fused_computation.2 | convolution fusion | flops 403046400 | bytes 17965056 | tf_op jit(solution)/shard_map/svrp,svpk->svrk/dot_general | solution.py:372
  15.5 24.3 %share.1 = (f32[2,72,512]{2,1,0:T(8,128)}, f32[2,24,512]{2,1,0:T(8,128)}, f32[8,128]{1,0:T(8,128)}) custom-call(s32[2]{0:T(128)} %bitcast.14, s32[2,3]{1,0:T(2,128)} %bitcast.15, f32[2,4,24,512]{3,2,1,0:T(8,128)} %fusion.1.refs_2_, f32[2,4,2048]{2,1,0:T(4,128)} %fusion.refs_3_), custom_call_target="tpu_custom_call" | custom-call | tf_op jit(solution)/shard_map/share/pallas_call | solution.py:341
  39.8 0.0 copy-start
  39.8 1.0 %copy-done = f32[2,72,512]{2,1,0:T(8,128)S(1)} copy-done((f32[2,72,512]{2,1,0:T(8,128)S(1)}, f32[2,72,512]{2,1,0:T(8,128)}, u32[]{:S(2)}) %copy-start) | copy-done | bytes 294936
  40.7 0.0 copy-start.1
  40.7 0.9 %copy-done.1 = f32[2,24,512]{2,1,0:T(8,128)S(1)} copy-done((f32[2,24,512]{2,1,0:T(8,128)S(1)}, f32[2,24,512]{2,1,0:T(8,128)}, u32[]{:S(2)}) %copy-start.1) | copy-done | bytes 98328
  41.6 0.0 copy-start.2
  41.6 0.7 %copy-done.2 = f32[8,128]{1,0:T(8,128)S(1)} copy-done((f32[8,128]{1,0:T(8,128)S(1)}, f32[8,128]{1,0:T(8,128)}, u32[]{:S(2)}) %copy-start.2) | copy-done | bytes 4120
  42.3 22.1 %fit.1 = (f32[2,24,397]{2,1,0:T(8,128)}, f32[2,24,512]{2,1,0:T(8,128)}) custom-call(f32[8,128]{1,0:T(8,128)S(1)} %copy-done.2, f32[2,24,512]{2,1,0:T(8,128)S(1)} %copy-done.1, f32[2,72,512]{2,1,0:T(8,128)S(1)} %copy-done), custom_call_target="tpu_custom_call" | custom-call | tf_op jit(solution)/shard_map/fit/pallas_call | solution.py:204
Async XLA Ops:
  0.6 10.7 %copy-start.3 = (bf16[1,2,4,2048,512]{4,3,2,1,0:T(8,128)(2,1)S(1)}, bf16[1,2,4,2048,512]{4,3,2,1,0:T(8,128)(2,1)}, u32[]{:S(2)}) copy-start(bf16[1,2,4,2048,512]{4,3,2,1,0:T(8,128)(2,1)} %param.4) | copy-start | bytes 50331652
  39.8 1.0 %copy-start = (f32[2,72,512]{2,1,0:T(8,128)S(1)}, f32[2,72,512]{2,1,0:T(8,128)}, u32[]{:S(2)}) copy-start(f32[2,72,512]{2,1,0:T(8,128)} %get-tuple-element.9.near_ref) | copy-start | bytes 884740
  40.7 0.9 %copy-start.1 = (f32[2,24,512]{2,1,0:T(8,128)S(1)}, f32[2,24,512]{2,1,0:T(8,128)}, u32[]{:S(2)}) copy-start(f32[2,24,512]{2,1,0:T(8,128)} %get-tuple-element.8.state_ref) | copy-start | bytes 294916
  41.6 0.7 %copy-start.2 = (f32[8,128]{1,0:T(8,128)S(1)}, f32[8,128]{1,0:T(8,128)}, u32[]{:S(2)}) copy-start(f32[8,128]{1,0:T(8,128)} %get-tuple-element.7.gnorm_ref) | copy-start | bytes 12292

commit v2 on v1

v2 whole, which is shorter than its diff:
```python
import jax
import jax.numpy as jnp
from jax import lax
from jax.experimental import pallas as pl
from jax.experimental.pallas import tpu as pltpu
from jax.sharding import PartitionSpec as P

beta_linear = 0.5
beta_quad = 0.5
LANES = 128
SUB = 8
STEP = 16
join = 2


def split3(a):
    hi = a.astype(jnp.bfloat16)
    left = a - hi.astype(jnp.float32)
    mid = left.astype(jnp.bfloat16)
    low = (left - mid.astype(jnp.float32)).astype(jnp.bfloat16)
    return hi, mid, low


def as_left(parts):
    hi, mid, low = parts
    return jnp.concatenate([hi, mid, hi, mid, hi, low], axis=1)


def as_right(parts, axis=1):
    hi, mid, low = parts
    return jnp.concatenate([hi, mid, mid, hi, low, hi], axis=axis)


def dot_nt(a, b):
    return lax.dot_general(a, b, (((1,), (1,)), ((), ())), preferred_element_type=jnp.float32)


def dot_nn(a, b):
    return jnp.dot(a, b, preferred_element_type=jnp.float32)


def pick(tile, index):
    rows = [
        jnp.take_along_axis(tile[r : r + SUB], index, axis=1, mode="promise_in_bounds")
        for r in range(0, tile.shape[0], SUB)
    ]
    return rows[0] if len(rows) == 1 else jnp.concatenate(rows, axis=0)


def whiten(block, wide):
    size = block.shape[0]
    lane8 = lax.broadcasted_iota(jnp.int32, (SUB, LANES), 1)
    half = lane8 - lane8 % wide
    lane = lax.broadcasted_iota(jnp.int32, (1, LANES), 1) % wide
    done = []
    rest = block
    for base in range(0, size, STEP):
        row = lax.broadcasted_iota(jnp.int32, (STEP, LANES), 0)
        inside = (lane >= base) & (lane < base + STEP)
        here = rest[0:STEP]
        rest = rest[STEP:]
        cols = jnp.stack([pick(here, half + (base + j)) for j in range(STEP)])
        side = [pick(rest, half + (base + j)) for j in range(STEP)] if rest.shape[0] else None
        here = jnp.where(inside, (lane - base == row).astype(jnp.float32), here)
        scaled = jnp.zeros((STEP, LANES), jnp.float32)
        for j in range(STEP):
            col = cols[0]
            inv = 1.0 / col[j : j + 1]
            now = here[j : j + 1]
            scaled = jnp.where(row == j, now * lax.rsqrt(col[j : j + 1]), scaled)
            now = now * inv
            here = jnp.where(row == j, now, here - col * now)
            if j + 1 < STEP:
                cols = cols[1:]
                top = cols[:, j : j + 1, :] * inv
                cols = jnp.where(row == j, top, cols - col * top)
        done.append(jnp.where(lane < base + STEP, scaled, 0.0))
        if rest.shape[0]:
            terms = [side[j] * here[j : j + 1] for j in range(STEP)]
            while len(terms) > 1:
                terms = [a + b for a, b in zip(terms[::2], terms[1::2])]
            rest = jnp.where(inside, 0.0, rest) - terms[0]
    return done[0] if len(done) == 1 else jnp.concatenate(done, axis=0)


def shape_of(subs, ranks, near):
    wide = LANES // subs
    nself = 1 + ranks + ranks * (ranks + 1) // 2
    nf = nself + near
    full = nf // wide
    early = nself // wide
    rest = -(-(nf - full * wide) // STEP) * STEP
    return wide, nself, nf, full, early, rest, full * wide + ranks + rest


def fit_body(gnorm, state_of, near_of, out_ref, f_ref, part_refs, subs, ranks, near, steps):
    wide, nself, nf, full, early, rest, tall = shape_of(subs, ranks, near)
    head = early * wide
    late = head + ranks
    keep = (lax.broadcasted_iota(jnp.int32, (1, steps), 1) < steps - 1).astype(jnp.float32)

    def place(s, first, size):
        for ref, part in zip(part_refs, split3(f_ref[s, first : first + size, :])):
            ref[s, first : first + size, :] = part

    tailing = []
    for s in range(subs):
        state = state_of(s)
        past = state * keep
        f_ref[s, 0:ranks, :] = past
        at = ranks
        for first in range(ranks):
            rows = past[first : first + 1] * state[first:]
            cut = max(0, min(ranks - first, head - at))
            if cut:
                f_ref[s, at : at + cut, :] = rows[:cut]
            if cut < ranks - first:
                tailing_at = at + cut - head + late
                f_ref[s, tailing_at : tailing_at + ranks - first - cut, :] = rows[cut:]
            at += ranks - first
        f_ref[s, head:late, :] = pltpu.roll(state, steps - 1, 1)
        f_ref[s, late + nself - 1 - head : late + nself - head, :] = keep
        place(s, 0, late)

    linear = beta_linear * gnorm * steps
    square = beta_quad * gnorm * gnorm * steps

    def ridge(first, size):
        row = lax.broadcasted_iota(jnp.int32, (size, LANES), 0)
        col = lax.broadcasted_iota(jnp.int32, (size, LANES), 1) % wide
        at = row + first
        level = jnp.where((at < ranks) | (at >= nself - 1), linear, square)
        level = jnp.where(at < nf, level, 1.0)
        return jnp.where(row == col, level, 0.0)

    def rows_at(j):
        return j * wide if j < early else late + (j - early) * wide

    def size_of(j):
        return wide if j < full else rest

    def gram(first, size, j):
        at, span = rows_at(j), size_of(j)
        total = None
        for s in range(subs):
            left = as_left([r[s, first : first + size, :] for r in part_refs])
            parts = []
            for r in part_refs:
                pieces = [r[s, at : at + span, :]]
                if s * wide:
                    pieces.insert(0, jnp.zeros((s * wide, steps), r.dtype))
                if LANES - s * wide - span:
                    pieces.append(jnp.zeros((LANES - s * wide - span, steps), r.dtype))
                parts.append(jnp.concatenate(pieces, axis=0))
            one = dot_nt(left, as_right(parts))
            total = one if total is None else total + one
        return total

    lanes = lax.broadcasted_iota(jnp.int32, (1, LANES), 1) // wide

    def pair(block):
        if block.shape[0] < wide:
            block = jnp.concatenate([block, jnp.zeros((wide - block.shape[0], LANES), block.dtype)], axis=0)
        return jnp.concatenate([jnp.where(lanes == s, block, 0.0) for s in range(subs)], axis=0)

    roots, tops, sides, lefts, boths = {}, {}, {}, {}, {}

    def extent(j, part):
        if part == 1:
            return (max(late, rows_at(j) + wide), tall)
        return (rows_at(j) + wide, late) if j < early else (head, late)

    def cut(table, k, first, last):
        part = int(first >= late)
        start = extent(k, part)[0]
        return table[k, part][first - start : last - start]

    def both(k, j):
        if (k, j) not in boths:
            block = cut(sides, k, rows_at(j), rows_at(j) + size_of(j))
            boths[k, j] = as_right(split3(pair(block)))
        return boths[k, j]

    def less(value, j, first, last, before):
        for k in before:
            value = value - dot_nt(cut(lefts, k, first, last), both(k, j))
        return value

    def top_of(j, before):
        if j not in tops:
            tops[j] = gram(rows_at(j), size_of(j), j) + ridge(j * wide, size_of(j))
        first = rows_at(j)
        tops[j] = less(tops[j], j, first, first + size_of(j), before)

    lows = {}

    def low_of(j, part, before):
        first, last = extent(j, part)
        if last > first:
            if (j, part) not in lows:
                lows[j, part] = gram(first, last - first, j)
            lows[j, part] = less(lows[j, part], j, first, last, before)

    def settle(j, part):
        if (j, part) in lows:
            side = dot_nt(as_left(split3(lows[j, part])), as_right(roots[j]))
            sides[j, part] = side
            lefts[j, part] = as_left(split3(side))

    def bring():
        for s in range(subs):
            there = near_of(s) * keep
            at = late + nself - head
            f_ref[s, at : at + near, :] = there
            f_ref[s, at + near : tall, :] = jnp.zeros((tall - at - near, steps), jnp.float32)
            place(s, late, tall - late)

    top_of(0, ())
    low_of(0, 0, ())
    for k in range(full + 1):
        if k == join:
            bring()
            for j in range(join):
                low_of(j, 1, range(j))
                settle(j, 1)
        roots[k] = split3(pair(whiten(tops[k], wide)))
        after = k + 1 if k < full else None
        if k >= join:
            low_of(k, 1, range(k))
        if after is not None and (after < early or k >= join):
            top_of(after, range(k))
            low_of(after, 0, range(k))
        settle(k, 0)
        if k >= join:
            settle(k, 1)
        if after is not None:
            if after < early or k >= join:
                top_of(after, (k,))
                low_of(after, 0, (k,))
    answer = [None] * (full + 1)
    scaled = {}
    for key, left in lefts.items():
        scaled[key] = dot_nn(left, as_right(roots[key[0]], 0))
    for k in range(full, -1, -1):
        total = cut(scaled, k, head, late)
        for j in range(full, k, -1):
            block = cut(scaled, k, rows_at(j), rows_at(j) + size_of(j))
            total = total - dot_nn(as_left(split3(answer[j])), as_right(split3(pair(block)), 0))
        answer[k] = total
    for s in range(subs):
        def lanes_of(first, last):
            out = []
            while first < last:
                k = first // wide
                end = min(last, (k + 1) * wide)
                out.append(answer[k][:, s * wide + first - k * wide : s * wide + end - k * wide])
                first = end
            return out
        order = lanes_of(nself - 1, nself) + lanes_of(0, ranks) + lanes_of(nself, nf) + lanes_of(ranks, nself - 1)
        out_ref[s] = jnp.concatenate(order, axis=1)


def fit_kernel(gnorm_ref, state_ref, near_ref, out_ref, kept_ref, f_ref, *part_refs):
    subs, ranks, steps = state_ref.shape
    kept_ref[...] = state_ref[...]
    fit_body(gnorm_ref[0:1, 0:1], lambda s: state_ref[s], lambda s: near_ref[s], out_ref, f_ref, part_refs,
             subs, ranks, near_ref.shape[1], steps)


def fit(gnorm, states, near):
    subs, ranks, steps = states.shape
    wide, nself, nf, full, early, rest, tall = shape_of(subs, ranks, near.shape[1])
    vmem = pl.BlockSpec(memory_space=pltpu.VMEM)
    return pl.pallas_call(
        fit_kernel,
        out_shape=(
            jax.ShapeDtypeStruct((subs, ranks, nf), jnp.float32),
            jax.ShapeDtypeStruct(states.shape, jnp.float32),
        ),
        in_specs=[vmem, vmem, vmem],
        out_specs=(vmem, vmem),
        scratch_shapes=[pltpu.VMEM((subs, tall, steps), jnp.float32)]
        + [pltpu.VMEM((subs, tall, steps), jnp.bfloat16)] * 3,
        compiler_params=pltpu.CompilerParams(vmem_limit_bytes=40 * 2**20),
        name="fit",
    )(gnorm, states, near)


CHUNKS = 4
ROWS = 64


def everyone(sizes):
    nx, ny = sizes
    x, y = lax.axis_index("gx"), lax.axis_index("gy")

    def at(dx, dy):
        return (lax.rem(x + dx + nx, nx), lax.rem(y + dy + ny, ny))

    others = [at(dx, dy) for dx in range(nx) for dy in range(ny) if dx or dy]
    return x, y, at, others


def gather_kernel(sizes, subs, nvar, counts_ref, snaps_ref, basis_ref, stage):
    nx, ny = sizes
    snap_ref, base_ref, proj_ref, square_ref, row_ref, all_ref, snap_sems, base_sems, row_sems = stage
    count, slots, steps = snap_ref.shape
    ranks = base_ref.shape[1]
    part = slots // CHUNKS
    x, y, at, others = everyone(sizes)

    def piece(i, c):
        span = pl.ds(c * part, part)
        return pltpu.make_async_copy(snaps_ref.at[i, span], snap_ref.at[i, span], snap_sems.at[i, c])

    def modes(i):
        return pltpu.make_async_copy(basis_ref.at[i], base_ref.at[i], base_sems.at[i])

    for i in range(count):
        modes(i).start()
        for c in range(CHUNKS):
            piece(i, c).start()
    barrier = pltpu.get_barrier_semaphore()
    for other in others:
        pl.semaphore_signal(barrier, inc=1, device_id=other, device_id_type=pl.DeviceIdType.MESH)

    def project(i, carry):
        live = counts_ref[i // nvar]
        modes(i).wait()
        lane = lax.broadcasted_iota(jnp.int32, (1, slots), 1)
        mask = jnp.where(lane < live, 1.0, 0.0).astype(jnp.bfloat16)
        masked = base_ref[i] * mask
        total = jnp.zeros((ranks, steps), jnp.float32)
        squares = jnp.zeros((SUB, LANES), jnp.float32)
        for c in range(CHUNKS):
            piece(i, c).wait()
            total = total + jnp.dot(
                masked[:, c * part : (c + 1) * part],
                snap_ref[i, c * part : (c + 1) * part, :],
                preferred_element_type=jnp.float32,
            )
            for first in range(c * part, (c + 1) * part, ROWS):
                value = snap_ref[i, first : first + ROWS, :].astype(jnp.float32)
                value = value * value
                value = sum(value[:, k : k + LANES] for k in range(0, steps, LANES))
                node = lax.broadcasted_iota(jnp.int32, (ROWS, LANES), 0) + first
                value = jnp.where(node < live, value, 0.0)
                squares = squares + jnp.sum(value.reshape(ROWS // SUB, SUB, LANES), axis=0)
        proj_ref[i] = total
        square_ref[i] = squares
        return carry

    lax.fori_loop(0, count, project, 0)

    pairs = [(v, w) for v in range(nvar) for w in range(v, nvar)]
    rows = []
    for v in range(nvar):
        rows.append(sum(square_ref[s * nvar + v] for s in range(subs)))
    for v, w in pairs:
        both = sum(proj_ref[s * nvar + v] * proj_ref[s * nvar + w] for s in range(subs))
        both = sum(both[:, k : k + LANES] for k in range(0, steps, LANES))
        rows.append(jnp.sum(both.reshape(ranks // SUB, SUB, LANES), axis=0))
    nodes = counts_ref[0]
    for s in range(1, subs):
        nodes = nodes + counts_ref[s]
    tall = -(-len(rows) // SUB) * SUB
    index = lax.broadcasted_iota(jnp.int32, (tall, LANES), 0)
    lane = lax.broadcasted_iota(jnp.int32, (tall, LANES), 1)
    table = jnp.zeros((tall, LANES), jnp.float32)
    for i, row in enumerate(rows):
        table = jnp.where(index == i, jnp.sum(row, axis=0, keepdims=True), table)
    table = jnp.broadcast_to(jnp.sum(table, axis=1, keepdims=True), table.shape)
    table = jnp.sum(jnp.where(index == lane, table, 0.0), axis=0, keepdims=True)
    row = jnp.where(lane[0:1] == len(rows), nodes.astype(jnp.float32), table)
    me = x * ny + y
    row_ref[0] = row
    all_ref[me] = row
    pl.semaphore_wait(barrier, len(others))
    sent = []
    for d, other in enumerate(others):
        copy = pltpu.make_async_remote_copy(
            src_ref=row_ref.at[0],
            dst_ref=all_ref.at[me],
            send_sem=row_sems.at[0, d],
            recv_sem=row_sems.at[1, d],
            device_id=other,
            device_id_type=pl.DeviceIdType.MESH,
        )
        copy.start()
        sent.append(copy)
    for copy in sent:
        copy.wait_recv()
    total = jnp.sum(all_ref[...], axis=0)
    stat = [jnp.broadcast_to(total[:, i : i + 1], (1, LANES)) for i in range(len(rows) + 1)]
    nodes = stat[len(rows)]
    scale = [jnp.sqrt(stat[v] / (nodes * steps) + 1e-06) for v in range(nvar)]
    inverse = [1.0 / part for part in scale]
    gnorm = jnp.zeros((1, LANES), jnp.float32)
    for i, (v, w) in enumerate(pairs):
        gnorm += (1.0 if v == w else 2.0) * stat[nvar + i] * (inverse[v] * inverse[w])
    gnorm = gnorm / (nx * ny * subs * ranks * steps)
    states = []
    for s in range(subs):
        state = proj_ref[s * nvar] * inverse[0][:, 0:1]
        for v in range(1, nvar):
            state = state + proj_ref[s * nvar + v] * inverse[v][:, 0:1]
        states.append(state)
    return gnorm, states, sent


class Halo:
    def __init__(self, sizes, subs, cell_ref, sems):
        nx, ny = sizes
        x, y, at, others = everyone(sizes)
        wide = subs + 2
        self.x, self.y, self.ny, self.subs, self.wide, self.cells = x, y, ny, subs, wide, cell_ref
        self.copies = []
        sides = [(dx, dy) for dx in (-1, 0, 1) for dy in (-1, 0, 1) if dx or dy]
        for i, (dx, dy) in enumerate(sides):
            first, size = (0, subs) if dy == 0 else ((subs - 1, 1) if dy > 0 else (0, 1))
            into = (1 - dx) * wide + (1 if dy == 0 else (0 if dy > 0 else subs + 1))
            copy = pltpu.make_async_remote_copy(
                src_ref=cell_ref.at[pl.ds(wide + 1 + first, size)],
                dst_ref=cell_ref.at[pl.ds(into, size)],
                send_sem=sems.at[0, i],
                recv_sem=sems.at[1, i],
                device_id=at(dx, dy),
                device_id_type=pl.DeviceIdType.MESH,
            )
            sends = (x + dx >= 0) & (x + dx < nx) & (y + dy >= 0) & (y + dy < ny)
            takes = (x - dx >= 0) & (x - dx < nx) & (y - dy >= 0) & (y - dy < ny)
            self.copies.append((copy, sends, takes))

    def start(self, states):
        for s, state in enumerate(states):
            self.cells[self.wide + 1 + s] = state
        for copy, sends, takes in self.copies:
            pl.when(sends)(copy.start)

    def arrive(self):
        for copy, sends, takes in self.copies:
            pl.when(takes)(copy.wait_recv)

    def finish(self):
        for copy, sends, takes in self.copies:
            pl.when(sends)(copy.wait_send)

    def near(self, links_ref, s):
        columns = self.ny * self.subs
        found = []
        for b in range(links_ref.shape[1]):
            link = links_ref[s, b]
            row = link // columns
            cell = (row - self.x + 1) * self.wide + link - row * columns - self.y * self.subs + 1
            found.append(self.cells[jnp.clip(cell, 0, 3 * self.wide - 1)])
        return found


def share_kernel(sizes, subs, nvar, counts_ref, links_ref, snaps_ref, basis_ref, near_ref, state_ref, gnorm_ref, cell_ref, halo_sems, *stage):
    ranks = state_ref.shape[1]
    gnorm, states, sent = gather_kernel(sizes, subs, nvar, counts_ref, snaps_ref, basis_ref, stage)
    halo = Halo(sizes, subs, cell_ref, halo_sems)
    halo.start(states)
    gnorm_ref[...] = jnp.broadcast_to(gnorm, gnorm_ref.shape)
    for s in range(subs):
        state_ref[s] = states[s]
    halo.arrive()
    for s in range(subs):
        for b, found in enumerate(halo.near(links_ref, s)):
            near_ref[s, b * ranks : b * ranks + ranks, :] = found
    for copy in sent:
        copy.wait_send()
    halo.finish()


def stage_shapes(devices, count, slots, ranks, steps):
    return [
        pltpu.VMEM((count, slots, steps), jnp.bfloat16),
        pltpu.VMEM((count, ranks, slots), jnp.bfloat16),
        pltpu.VMEM((count, ranks, steps), jnp.float32),
        pltpu.VMEM((count, SUB, LANES), jnp.float32),
        pltpu.VMEM((1, 1, LANES), jnp.float32),
        pltpu.VMEM((devices, 1, LANES), jnp.float32),
        pltpu.SemaphoreType.DMA((count, CHUNKS)),
        pltpu.SemaphoreType.DMA((count,)),
        pltpu.SemaphoreType.DMA((2, devices - 1)),
    ]


def share(counts, links, snaps, basis):
    nx, ny = lax.axis_size("gx"), lax.axis_size("gy")
    subs, nvar, ranks, slots = basis.shape
    steps = snaps.shape[3]
    smem = pl.BlockSpec(memory_space=pltpu.SMEM)
    vmem = pl.BlockSpec(memory_space=pltpu.VMEM)
    hbm = pl.BlockSpec(memory_space=pltpu.HBM)

    def kernel(*refs):
        share_kernel((nx, ny), subs, nvar, *refs)

    return pl.pallas_call(
        kernel,
        out_shape=(
            jax.ShapeDtypeStruct((subs, links.shape[1] * ranks, steps), jnp.float32),
            jax.ShapeDtypeStruct((subs, ranks, steps), jnp.float32),
            jax.ShapeDtypeStruct((SUB, LANES), jnp.float32),
        ),
        in_specs=[smem, smem, hbm, hbm],
        out_specs=(vmem, vmem, vmem),
        scratch_shapes=[
            pltpu.VMEM((3 * (subs + 2), ranks, steps), jnp.float32),
            pltpu.SemaphoreType.DMA((2, 8)),
        ]
        + stage_shapes(nx * ny, subs * nvar, slots, ranks, steps),
        compiler_params=pltpu.CompilerParams(collective_id=0, has_side_effects=True, vmem_limit_bytes=60 * 2**20),
        name="share",
    )(counts, links, snaps.reshape(subs * nvar, slots, steps), basis.reshape(subs * nvar, ranks, slots))


def body(snapshots, basis, node_counts, adjacency):
    near, states, gnorm = share(node_counts[0], adjacency[0], snapshots[0], basis[0])
    operator, states = fit(gnorm, states, near)
    return (operator.swapaxes(1, 2)[None], states[None])


def solution(mesh):
    in_specs = (
        P("gx", "gy", None, None, None),
        P("gx", "gy", None, None, None),
        P("gx", "gy"),
        P("gx", "gy", None),
    )
    out_specs = (P("gx", "gy", None, None), P("gx", "gy", None, None))
    return jax.shard_map(body, mesh=mesh, in_specs=in_specs, out_specs=out_specs, check_vma=False)
```

time: 64.7 us -> 52.1 us (0.81)
  other arithmetic: 9.09 us -> 0 us
  matrix products: 4.18 us -> 0 us
  Pallas kernels: 46.3 us -> 48.7 us
  local copies, waits for them, and re-layouts: 4.12 us -> 2.53 us
    dot_general x1 -> x0, other arithmetic: 8.21 us -> none  [body(): jnp.einsum('svpk,svpk->svp', values, values, preferred_element_type=jnp.f...]
    pallas_call x1, Pallas kernels: 24.3 us -> 30.5 us  [share(): pl.pallas_call(kernel, out_shape=(jax.ShapeDtypeStruct((subs, links.shape...]
    dot_general x1 -> x0, matrix products: 4.18 us -> none  [body(): jnp.einsum('svrp,svpk->svrk', masked, values, preferred_element_type=jnp....]
    pallas_call x1, Pallas kernels: 22.1 us -> 18.2 us  [fit(): pl.pallas_call(fit_kernel, out_shape=(jax.ShapeDtypeStruct((subs, ranks,...]
    unnamed x8 -> x6, local copies, waits for them, and re-layouts: 4.12 us -> 2.53 us
    convert_element_type x1 -> x0, other arithmetic: 0.88 us -> none  [body(): masked = modes * live.astype(jnp.bfloat16)[:, None, None, :]]
where the time goes in v2:
time: 52.1 us; the launch traced here: 51.9 us
  Pallas kernels  48.7 us (93%)
  local copies, waits for them, and re-layouts  2.53 us (5%)
  between operations  0.65 us (1%)
    pallas_call x1, Pallas kernels, share(): pl.pallas_call(kernel, out_shape=(jax.ShapeDtypeStruct((subs, links.shape...  30.5 us
    pallas_call x1, Pallas kernels, fit(): pl.pallas_call(fit_kernel, out_shape=(jax.ShapeDtypeStruct((subs, ranks,...  18.2 us
    unnamed x6, local copies, waits for them, and re-layouts  2.53 us

profile of v2, /device:TPU:0, one launch (start us, length us, event | category | flops | bytes accessed | tf_op | source)
XLA Modules:
  0.0 51.9 jit_solution(17520639032278746727)
XLA Ops:
  0.6 30.5 %share.1 = (f32[2,72,512]{2,1,0:T(8,128)}, f32[2,24,512]{2,1,0:T(8,128)}, f32[8,128]{1,0:T(8,128)}) custom-call(s32[2]{0:T(128)} %bitcast.11, s32[2,3]{1,0:T(2,128)} %bitcast.10, bf16[8,2048,512]{2,1,0:T(8,128)(2,1)} %bitcast.8, bf16[8,24,2048]{2,1,0:T(8,128)(2,1)} %bitcast.9), custom_call_target="tpu_custom_call" | custom-call | tf_op jit(solution)/shard_map/share/pallas_call | solution.py:501
  31.2 0.0 copy-start
  31.2 1.0 %copy-done = f32[2,72,512]{2,1,0:T(8,128)S(1)} copy-done((f32[2,72,512]{2,1,0:T(8,128)S(1)}, f32[2,72,512]{2,1,0:T(8,128)}, u32[]{:S(2)}) %copy-start) | copy-done | bytes 294936
  32.1 0.0 copy-start.1
  32.1 0.9 %copy-done.1 = f32[2,24,512]{2,1,0:T(8,128)S(1)} copy-done((f32[2,24,512]{2,1,0:T(8,128)S(1)}, f32[2,24,512]{2,1,0:T(8,128)}, u32[]{:S(2)}) %copy-start.1) | copy-done | bytes 98328
  33.0 0.0 copy-start.2
  33.0 0.7 %copy-done.2 = f32[8,128]{1,0:T(8,128)S(1)} copy-done((f32[8,128]{1,0:T(8,128)S(1)}, f32[8,128]{1,0:T(8,128)}, u32[]{:S(2)}) %copy-start.2) | copy-done | bytes 4120
  33.7 18.2 %fit.1 = (f32[2,24,397]{2,1,0:T(8,128)}, f32[2,24,512]{2,1,0:T(8,128)}) custom-call(f32[8,128]{1,0:T(8,128)S(1)} %copy-done.2, f32[2,24,512]{2,1,0:T(8,128)S(1)} %copy-done.1, f32[2,72,512]{2,1,0:T(8,128)S(1)} %copy-done), custom_call_target="tpu_custom_call" | custom-call | tf_op jit(solution)/shard_map/fit/pallas_call | solution.py:274
Async XLA Ops:
  31.2 1.0 %copy-start = (f32[2,72,512]{2,1,0:T(8,128)S(1)}, f32[2,72,512]{2,1,0:T(8,128)}, u32[]{:S(2)}) copy-start(f32[2,72,512]{2,1,0:T(8,128)} %get-tuple-element.9.near_ref) | copy-start | bytes 884740
  32.1 0.9 %copy-start.1 = (f32[2,24,512]{2,1,0:T(8,128)S(1)}, f32[2,24,512]{2,1,0:T(8,128)}, u32[]{:S(2)}) copy-start(f32[2,24,512]{2,1,0:T(8,128)} %get-tuple-element.8.state_ref) | copy-start | bytes 294916
  33.0 0.7 %copy-start.2 = (f32[8,128]{1,0:T(8,128)S(1)}, f32[8,128]{1,0:T(8,128)}, u32[]{:S(2)}) copy-start(f32[8,128]{1,0:T(8,128)} %get-tuple-element.7.gnorm_ref) | copy-start | bytes 12292

commit v3 on v2

--- a/solution.py
+++ b/solution.py
@@ -39,9 +39,14 @@
     return jnp.dot(a, b, preferred_element_type=jnp.float32)
 
 
+ALONG = lax.GatherDimensionNumbers(
+    offset_dims=(), collapsed_slice_dims=(1,), start_index_map=(1,), operand_batching_dims=(0,), start_indices_batching_dims=(0,)
+)
+
+
 def pick(tile, index):
     rows = [
-        jnp.take_along_axis(tile[r : r + SUB], index, axis=1, mode="promise_in_bounds")
+        lax.gather(tile[r : r + SUB], index, ALONG, (1, 1), mode=lax.GatherScatterMode.PROMISE_IN_BOUNDS)
         for r in range(0, tile.shape[0], SUB)
     ]
     return rows[0] if len(rows) == 1 else jnp.concatenate(rows, axis=0)
@@ -59,8 +64,9 @@
         inside = (lane >= base) & (lane < base + STEP)
         here = rest[0:STEP]
         rest = rest[STEP:]
-        cols = jnp.stack([pick(here, half + (base + j)) for j in range(STEP)])
-        side = [pick(rest, half + (base + j)) for j in range(STEP)] if rest.shape[0] else None
+        index = [(half + (base + j))[:, :, None] for j in range(STEP)]
+        cols = jnp.stack([pick(here, index[j]) for j in range(STEP)])
+        side = [pick(rest, index[j]) for j in range(STEP)] if rest.shape[0] else None
         here = jnp.where(inside, (lane - base == row).astype(jnp.float32), here)
         scaled = jnp.zeros((STEP, LANES), jnp.float32)
         for j in range(STEP):
@@ -93,7 +99,7 @@
     return wide, nself, nf, full, early, rest, full * wide + ranks + rest
 
 
-def fit_body(gnorm, state_of, near_of, out_ref, f_ref, part_refs, subs, ranks, near, steps):
+def fit_body(gnorm, state_of, near_of, arrive, out_ref, f_ref, part_refs, subs, ranks, near, steps):
     wide, nself, nf, full, early, rest, tall = shape_of(subs, ranks, near)
     head = early * wide
     late = head + ranks
@@ -208,6 +214,7 @@
             lefts[j, part] = as_left(split3(side))
 
     def bring():
+        arrive()
         for s in range(subs):
             there = near_of(s) * keep
             at = late + nself - head
@@ -258,32 +265,6 @@
             return out
         order = lanes_of(nself - 1, nself) + lanes_of(0, ranks) + lanes_of(nself, nf) + lanes_of(ranks, nself - 1)
         out_ref[s] = jnp.concatenate(order, axis=1)
-
-
-def fit_kernel(gnorm_ref, state_ref, near_ref, out_ref, kept_ref, f_ref, *part_refs):
-    subs, ranks, steps = state_ref.shape
-    kept_ref[...] = state_ref[...]
-    fit_body(gnorm_ref[0:1, 0:1], lambda s: state_ref[s], lambda s: near_ref[s], out_ref, f_ref, part_refs,
-             subs, ranks, near_ref.shape[1], steps)
-
-
-def fit(gnorm, states, near):
-    subs, ranks, steps = states.shape
-    wide, nself, nf, full, early, rest, tall = shape_of(subs, ranks, near.shape[1])
-    vmem = pl.BlockSpec(memory_space=pltpu.VMEM)
-    return pl.pallas_call(
-        fit_kernel,
-        out_shape=(
-            jax.ShapeDtypeStruct((subs, ranks, nf), jnp.float32),
-            jax.ShapeDtypeStruct(states.shape, jnp.float32),
-        ),
-        in_specs=[vmem, vmem, vmem],
-        out_specs=(vmem, vmem),
-        scratch_shapes=[pltpu.VMEM((subs, tall, steps), jnp.float32)]
-        + [pltpu.VMEM((subs, tall, steps), jnp.bfloat16)] * 3,
-        compiler_params=pltpu.CompilerParams(vmem_limit_bytes=40 * 2**20),
-        name="fit",
-    )(gnorm, states, near)
 
 
 CHUNKS = 4
@@ -456,18 +437,19 @@
         return found
 
 
-def share_kernel(sizes, subs, nvar, counts_ref, links_ref, snaps_ref, basis_ref, near_ref, state_ref, gnorm_ref, cell_ref, halo_sems, *stage):
-    ranks = state_ref.shape[1]
+def solve_kernel(sizes, subs, nvar, counts_ref, links_ref, snaps_ref, basis_ref, out_ref, state_ref, cell_ref, f_ref, hi_ref, mid_ref, low_ref, halo_sems, *stage):
+    ranks, steps = state_ref.shape[1:]
     gnorm, states, sent = gather_kernel(sizes, subs, nvar, counts_ref, snaps_ref, basis_ref, stage)
     halo = Halo(sizes, subs, cell_ref, halo_sems)
     halo.start(states)
-    gnorm_ref[...] = jnp.broadcast_to(gnorm, gnorm_ref.shape)
     for s in range(subs):
         state_ref[s] = states[s]
-    halo.arrive()
-    for s in range(subs):
-        for b, found in enumerate(halo.near(links_ref, s)):
-            near_ref[s, b * ranks : b * ranks + ranks, :] = found
+
+    def near_of(s):
+        return jnp.concatenate(halo.near(links_ref, s), axis=0)
+
+    fit_body(gnorm[:, 0:1], lambda s: state_ref[s], near_of, halo.arrive, out_ref, f_ref, (hi_ref, mid_ref, low_ref),
+             subs, ranks, links_ref.shape[1] * ranks, steps)
     for copy in sent:
         copy.wait_send()
     halo.finish()
@@ -487,39 +469,42 @@
     ]
 
 
-def share(counts, links, snaps, basis):
+def solve(counts, links, snaps, basis):
     nx, ny = lax.axis_size("gx"), lax.axis_size("gy")
     subs, nvar, ranks, slots = basis.shape
     steps = snaps.shape[3]
+    wide, nself, nf, full, early, rest, tall = shape_of(subs, ranks, links.shape[1] * ranks)
     smem = pl.BlockSpec(memory_space=pltpu.SMEM)
     vmem = pl.BlockSpec(memory_space=pltpu.VMEM)
     hbm = pl.BlockSpec(memory_space=pltpu.HBM)
 
     def kernel(*refs):
-        share_kernel((nx, ny), subs, nvar, *refs)
+        solve_kernel((nx, ny), subs, nvar, *refs)
 
     return pl.pallas_call(
         kernel,
         out_shape=(
-            jax.ShapeDtypeStruct((subs, links.shape[1] * ranks, steps), jnp.float32),
+            jax.ShapeDtypeStruct((subs, ranks, nf), jnp.float32),
             jax.ShapeDtypeStruct((subs, ranks, steps), jnp.float32),
-            jax.ShapeDtypeStruct((SUB, LANES), jnp.float32),
         ),
         in_specs=[smem, smem, hbm, hbm],
-        out_specs=(vmem, vmem, vmem),
+        out_specs=(vmem, vmem),
         scratch_shapes=[
             pltpu.VMEM((3 * (subs + 2), ranks, steps), jnp.float32),
+            pltpu.VMEM((subs, tall, steps), jnp.float32),
+            pltpu.VMEM((subs, tall, steps), jnp.bfloat16),
+            pltpu.VMEM((subs, tall, steps), jnp.bfloat16),
+            pltpu.VMEM((subs, tall, steps), jnp.bfloat16),
             pltpu.SemaphoreType.DMA((2, 8)),
         ]
         + stage_shapes(nx * ny, subs * nvar, slots, ranks, steps),
         compiler_params=pltpu.CompilerParams(collective_id=0, has_side_effects=True, vmem_limit_bytes=60 * 2**20),
-        name="share",
+        name="solve",
     )(counts, links, snaps.reshape(subs * nvar, slots, steps), basis.reshape(subs * nvar, ranks, slots))
 
 
 def body(snapshots, basis, node_counts, adjacency):
-    near, states, gnorm = share(node_counts[0], adjacency[0], snapshots[0], basis[0])
-    operator, states = fit(gnorm, states, near)
+    operator, states = solve(node_counts[0], adjacency[0], snapshots[0], basis[0])
     return (operator.swapaxes(1, 2)[None], states[None])
 
 

time: 52.1 us -> 46.1 us (0.88)
  the two profiles are of different devices: /device:TPU:0 before, /device:TPU:5 now
where the time goes in v3:
time: 46.1 us; the launch traced here: 45.9 us
  Pallas kernels  42.2 us (92%)
  local copies, waits for them, and re-layouts  3.08 us (7%)
  between operations  0.64 us (1%)
    pallas_call x1, Pallas kernels, solve(): pl.pallas_call(kernel, out_shape=(jax.ShapeDtypeStruct((subs, ranks, nf),...  42.2 us
    unnamed x2, local copies, waits for them, and re-layouts  3.08 us

profile of v3, /device:TPU:5, one launch (start us, length us, event | category | flops | bytes accessed | tf_op | source)
XLA Modules:
  0.0 45.9 jit_solution(10500138664077641342)
XLA Ops:
  0.6 42.2 %solve.1 = (f32[2,24,397]{2,1,0:T(8,128)}, f32[2,24,512]{2,1,0:T(8,128)}) custom-call(s32[2]{0:T(128)} %bitcast.13, s32[2,3]{1,0:T(2,128)} %bitcast.12, bf16[8,2048,512]{2,1,0:T(8,128)(2,1)} %bitcast.8, bf16[8,24,2048]{2,1,0:T(8,128)(2,1)} %bitcast.9), custom_call_target="tpu_custom_call" | custom-call | tf_op jit(solution)/shard_map/solve/pallas_call | solution.py:484
  42.8 1.5 %copy.8 = f32[1,2,397,24]{2,3,1,0:T(8,128)} copy(f32[1,2,397,24]{2,3,1,0:T(8,128)} %bitcast.11) | data formatting | bytes 152448
  44.3 1.5 %copy.9 = f32[1,2,24,512]{3,2,1,0:T(8,128)} copy(f32[1,2,24,512]{3,2,1,0:T(8,128)} %bitcast.10) | data formatting | bytes 196608

commit v4 on v3

--- a/solution.py
+++ b/solution.py
@@ -10,7 +10,7 @@
 LANES = 128
 SUB = 8
 STEP = 16
-join = 2
+join = 3
 
 
 def split3(a):
@@ -145,22 +145,37 @@
     def size_of(j):
         return wide if j < full else rest
 
+    products = {}
+
+    def product(rows, cols):
+        if (rows, cols) not in products:
+            products[rows, cols] = [
+                dot_nt(
+                    as_left([r[s, rows[0] : rows[1], :] for r in part_refs]),
+                    as_right([r[s, cols[0] : cols[1], :] for r in part_refs]),
+                )
+                for s in range(subs)
+            ]
+        return products[rows, cols]
+
+    group = 2 * LANES // wide
+
     def gram(first, size, j):
         at, span = rows_at(j), size_of(j)
-        total = None
-        for s in range(subs):
-            left = as_left([r[s, first : first + size, :] for r in part_refs])
-            parts = []
-            for r in part_refs:
-                pieces = [r[s, at : at + span, :]]
-                if s * wide:
-                    pieces.insert(0, jnp.zeros((s * wide, steps), r.dtype))
-                if LANES - s * wide - span:
-                    pieces.append(jnp.zeros((LANES - s * wide - span, steps), r.dtype))
-                parts.append(jnp.concatenate(pieces, axis=0))
-            one = dot_nt(left, as_right(parts))
-            total = one if total is None else total + one
-        return total
+        if j < early:
+            block = j - j % group
+            cols = (block * wide, min(block + group, early) * wide)
+            rows = (cols[0], cols[0] + wide) if first < cols[0] + wide else (cols[0] + wide, late)
+        else:
+            cols, rows = (late, tall), (head, late)
+        if first >= late:
+            rows = (late, tall)
+        pieces = []
+        for whole in product(rows, cols):
+            pieces.append(whole[first - rows[0] : first - rows[0] + size, at - cols[0] : at - cols[0] + span])
+            if span < wide:
+                pieces.append(jnp.zeros((size, wide - span), jnp.float32))
+        return jnp.concatenate(pieces, axis=1)
 
     lanes = lax.broadcasted_iota(jnp.int32, (1, LANES), 1) // wide
 
@@ -214,7 +229,6 @@
             lefts[j, part] = as_left(split3(side))
 
     def bring():
-        arrive()
         for s in range(subs):
             there = near_of(s) * keep
             at = late + nself - head
@@ -226,11 +240,13 @@
     low_of(0, 0, ())
     for k in range(full + 1):
         if k == join:
+            arrive()
+        roots[k] = split3(pair(whiten(tops[k], wide)))
+        if k == join:
             bring()
             for j in range(join):
                 low_of(j, 1, range(j))
                 settle(j, 1)
-        roots[k] = split3(pair(whiten(tops[k], wide)))
         after = k + 1 if k < full else None
         if k >= join:
             low_of(k, 1, range(k))
@@ -267,8 +283,8 @@
         out_ref[s] = jnp.concatenate(order, axis=1)
 
 
-CHUNKS = 4
-ROWS = 64
+CHUNKS = 1
+ROWS = 16
 
 
 def everyone(sizes):
@@ -503,8 +519,46 @@
     )(counts, links, snaps.reshape(subs * nvar, slots, steps), basis.reshape(subs * nvar, ranks, slots))
 
 
+def emit_kernel(first_ref, second_ref, out_ref, kept_ref, one_ref, two_ref, sems):
+    reads = [
+        pltpu.make_async_copy(first_ref, one_ref, sems.at[0]),
+        pltpu.make_async_copy(second_ref, two_ref, sems.at[1]),
+    ]
+    writes = [
+        pltpu.make_async_copy(one_ref, out_ref, sems.at[2]),
+        pltpu.make_async_copy(two_ref, kept_ref, sems.at[3]),
+    ]
+    for copy in reads:
+        copy.start()
+    for read, write in zip(reads, writes):
+        read.wait()
+        write.start()
+    for copy in writes:
+        copy.wait()
+
+
+def emit(first, second):
+    hbm = pl.BlockSpec(memory_space=pltpu.HBM)
+    return pl.pallas_call(
+        emit_kernel,
+        out_shape=(
+            jax.ShapeDtypeStruct(first.shape, first.dtype),
+            jax.ShapeDtypeStruct(second.shape, second.dtype),
+        ),
+        in_specs=[hbm, hbm],
+        out_specs=(hbm, hbm),
+        scratch_shapes=[
+            pltpu.VMEM(first.shape, first.dtype),
+            pltpu.VMEM(second.shape, second.dtype),
+            pltpu.SemaphoreType.DMA((4,)),
+        ],
+        name="emit",
+    )(first, second)
+
+
 def body(snapshots, basis, node_counts, adjacency):
     operator, states = solve(node_counts[0], adjacency[0], snapshots[0], basis[0])
+    operator, states = emit(operator, states)
     return (operator.swapaxes(1, 2)[None], states[None])
 
 

time: 46.1 us -> 40.5 us (0.88)
  the two profiles are of different devices: /device:TPU:5 before, /device:TPU:0 now
where the time goes in v4:
time: 40.5 us; the launch traced here: 40.3 us
  Pallas kernels  39.7 us (98%)
  between operations  0.64 us (2%)
    pallas_call x1, Pallas kernels, solve(): pl.pallas_call(kernel, out_shape=(jax.ShapeDtypeStruct((subs, ranks, nf),...  38 us
    pallas_call x1, Pallas kernels, emit(): pl.pallas_call(emit_kernel, out_shape=(jax.ShapeDtypeStruct(first.shape,...  1.61 us

profile of v4, /device:TPU:0, one launch (start us, length us, event | category | flops | bytes accessed | tf_op | source)
XLA Modules:
  0.0 40.3 jit_solution(4196828575290543124)
XLA Ops:
  0.6 38.0 %solve.1 = (f32[2,24,397]{2,1,0:T(8,128)}, f32[2,24,512]{2,1,0:T(8,128)}) custom-call(s32[2]{0:T(128)} %bitcast.11, s32[2,3]{1,0:T(2,128)} %bitcast.10, bf16[8,2048,512]{2,1,0:T(8,128)(2,1)} %bitcast.8, bf16[8,24,2048]{2,1,0:T(8,128)(2,1)} %bitcast.9), custom_call_target="tpu_custom_call" | custom-call | tf_op jit(solution)/shard_map/solve/pallas_call | solution.py:500
  38.7 1.6 %emit.1 = (f32[2,24,397]{2,1,0:T(8,128)}, f32[2,24,512]{2,1,0:T(8,128)}) custom-call(f32[2,24,397]{2,1,0:T(8,128)} %get-tuple-element.6.first_ref, f32[2,24,512]{2,1,0:T(8,128)} %get-tuple-element.7.second_ref), custom_call_target="tpu_custom_call" | custom-call | tf_op jit(solution)/shard_map/emit/pallas_call | solution.py:542

commit v5 on v4

--- a/solution.py
+++ b/solution.py
@@ -96,13 +96,13 @@
     full = nf // wide
     early = nself // wide
     rest = -(-(nf - full * wide) // STEP) * STEP
-    return wide, nself, nf, full, early, rest, full * wide + ranks + rest
+    return wide, nself, nf, full, early, rest, full * wide + -(-ranks // STEP) * STEP + rest
 
 
 def fit_body(gnorm, state_of, near_of, arrive, out_ref, f_ref, part_refs, subs, ranks, near, steps):
     wide, nself, nf, full, early, rest, tall = shape_of(subs, ranks, near)
     head = early * wide
-    late = head + ranks
+    late = head + -(-ranks // STEP) * STEP
     keep = (lax.broadcasted_iota(jnp.int32, (1, steps), 1) < steps - 1).astype(jnp.float32)
 
     def place(s, first, size):
@@ -124,7 +124,9 @@
                 tailing_at = at + cut - head + late
                 f_ref[s, tailing_at : tailing_at + ranks - first - cut, :] = rows[cut:]
             at += ranks - first
-        f_ref[s, head:late, :] = pltpu.roll(state, steps - 1, 1)
+        f_ref[s, head : head + ranks, :] = pltpu.roll(state, steps - 1, 1)
+        if late > head + ranks:
+            f_ref[s, head + ranks : late, :] = jnp.zeros((late - head - ranks, steps), jnp.float32)
         f_ref[s, late + nself - 1 - head : late + nself - head, :] = keep
         place(s, 0, late)
 
@@ -184,49 +186,97 @@
             block = jnp.concatenate([block, jnp.zeros((wide - block.shape[0], LANES), block.dtype)], axis=0)
         return jnp.concatenate([jnp.where(lanes == s, block, 0.0) for s in range(subs)], axis=0)
 
-    roots, tops, sides, lefts, boths = {}, {}, {}, {}, {}
+    roots, sides, lefts, boths, cols, tops, heads = {}, {}, {}, {}, {}, {}, {}
 
     def extent(j, part):
         if part == 1:
-            return (max(late, rows_at(j) + wide), tall)
-        return (rows_at(j) + wide, late) if j < early else (head, late)
-
-    def cut(table, k, first, last):
-        part = int(first >= late)
-        start = extent(k, part)[0]
-        return table[k, part][first - start : last - start]
+            return (max(late, rows_at(j)), tall)
+        return (rows_at(j), late) if j < early else (head, late)
+
+    def home(j):
+        return 0 if j < early else 1
+
+    def after(k, part):
+        first, last = extent(k, part)
+        return (first + size_of(k), last) if part == home(k) else (first, last)
+
+    def left_of(k, parts):
+        if (k, parts) not in lefts:
+            have = [sides[k, p] for p in parts if (k, p) in sides]
+            lefts[k, parts] = as_left(split3(have[0] if len(have) == 1 else jnp.concatenate(have, axis=0)))
+        return lefts[k, parts]
+
+    def index(k, parts, row):
+        base = 0
+        for p in parts:
+            first, last = after(k, p)
+            if first <= row < last:
+                return base + row - first
+            base += last - first
 
     def both(k, j):
         if (k, j) not in boths:
-            block = cut(sides, k, rows_at(j), rows_at(j) + size_of(j))
-            boths[k, j] = as_right(split3(pair(block)))
+            at = index(k, (home(j),), rows_at(j))
+            boths[k, j] = as_right(split3(pair(sides[k, home(j)][at : at + size_of(j)])))
         return boths[k, j]
 
-    def less(value, j, first, last, before):
+    def start(j, parts):
+        for part in parts:
+            if part == home(j):
+                tops[j] = gram(rows_at(j), size_of(j), j) + ridge(j * wide, size_of(j))
+            first, last = after(j, part)
+            if last > first:
+                cols[j, part] = gram(first, last - first, j)
+
+    def update(j, before, parts):
         for k in before:
-            value = value - dot_nt(cut(lefts, k, first, last), both(k, j))
-        return value
-
-    def top_of(j, before):
-        if j not in tops:
-            tops[j] = gram(rows_at(j), size_of(j), j) + ridge(j * wide, size_of(j))
-        first = rows_at(j)
-        tops[j] = less(tops[j], j, first, first + size_of(j), before)
-
-    lows = {}
-
-    def low_of(j, part, before):
-        first, last = extent(j, part)
-        if last > first:
-            if (j, part) not in lows:
-                lows[j, part] = gram(first, last - first, j)
-            lows[j, part] = less(lows[j, part], j, first, last, before)
-
-    def settle(j, part):
-        if (j, part) in lows:
-            side = dot_nt(as_left(split3(lows[j, part])), as_right(roots[j]))
-            sides[j, part] = side
-            lefts[j, part] = as_left(split3(side))
+            ahead = j == k + 1 and home(j) in parts
+            if ahead:
+                tops[j] = tops[j] - dot_nt(as_left(split3(heads[k])), both(k, j))
+            wanted = [after(j, p) for p in parts]
+            if home(j) in parts and not ahead:
+                wanted.append((rows_at(j), rows_at(j) + size_of(j)))
+            wanted = [w for w in wanted if w[1] > w[0]]
+            if not wanted:
+                continue
+            base = min(index(k, parts, w[0]) for w in wanted)
+            less = dot_nt(left_of(k, parts)[base:], both(k, j))
+            for part in parts:
+                low, high = after(j, part)
+                if high > low:
+                    at = index(k, parts, low) - base
+                    cols[j, part] = cols[j, part] - less[at : at + high - low]
+                if part == home(j) and not ahead:
+                    at = index(k, parts, rows_at(j)) - base
+                    tops[j] = tops[j] - less[at : at + size_of(j)]
+
+    def settle(k, parts):
+        lead = k < full and home(k + 1) in parts
+        rest = []
+        for part in parts:
+            if (k, part) in cols:
+                value = cols[k, part]
+                if lead and part == home(k + 1):
+                    size = size_of(k + 1)
+                    heads[k] = dot_nt(as_left(split3(value[:size])), as_right(roots[k]))
+                    boths[k, k + 1] = as_right(split3(pair(heads[k])))
+                    value = value[size:]
+                if value.shape[0]:
+                    rest.append((part, value))
+        done = {}
+        if rest:
+            value = rest[0][1] if len(rest) == 1 else jnp.concatenate([v for p, v in rest], axis=0)
+            side = dot_nt(as_left(split3(value)), as_right(roots[k]))
+            at = 0
+            for part, value in rest:
+                done[part] = side[at : at + value.shape[0]]
+                at += value.shape[0]
+        for part in parts:
+            pieces = [heads[k]] if lead and part == home(k + 1) else []
+            if part in done:
+                pieces.append(done[part])
+            if pieces:
+                sides[k, part] = pieces[0] if len(pieces) == 1 else jnp.concatenate(pieces, axis=0)
 
     def bring():
         for s in range(subs):
@@ -236,38 +286,33 @@
             f_ref[s, at + near : tall, :] = jnp.zeros((tall - at - near, steps), jnp.float32)
             place(s, late, tall - late)
 
-    top_of(0, ())
-    low_of(0, 0, ())
+    start(0, (0,))
     for k in range(full + 1):
         if k == join:
             arrive()
         roots[k] = split3(pair(whiten(tops[k], wide)))
         if k == join:
             bring()
-            for j in range(join):
-                low_of(j, 1, range(j))
-                settle(j, 1)
-        after = k + 1 if k < full else None
-        if k >= join:
-            low_of(k, 1, range(k))
-        if after is not None and (after < early or k >= join):
-            top_of(after, range(k))
-            low_of(after, 0, range(k))
-        settle(k, 0)
-        if k >= join:
-            settle(k, 1)
-        if after is not None:
-            if after < early or k >= join:
-                top_of(after, (k,))
-                low_of(after, 0, (k,))
+            for j in range(join + 1):
+                start(j, (1,))
+                update(j, range(j), (1,))
+                if j < join:
+                    settle(j, (1,))
+        parts = (0,) if k < join else (0, 1)
+        if k < full:
+            start(k + 1, parts)
+            update(k + 1, range(k), parts)
+        settle(k, parts)
+        if k < full:
+            update(k + 1, (k,), parts)
     answer = [None] * (full + 1)
-    scaled = {}
-    for key, left in lefts.items():
-        scaled[key] = dot_nn(left, as_right(roots[key[0]], 0))
+    scaled = [dot_nn(left_of(k, (0, 1)), as_right(roots[k], 0)) for k in range(full + 1)]
     for k in range(full, -1, -1):
-        total = cut(scaled, k, head, late)
+        at = index(k, (0, 1), head)
+        total = scaled[k][at : at + ranks]
         for j in range(full, k, -1):
-            block = cut(scaled, k, rows_at(j), rows_at(j) + size_of(j))
+            at = index(k, (0, 1), rows_at(j))
+            block = scaled[k][at : at + size_of(j)]
             total = total - dot_nn(as_left(split3(answer[j])), as_right(split3(pair(block)), 0))
         answer[k] = total
     for s in range(subs):
@@ -298,7 +343,7 @@
     return x, y, at, others
 
 
-def gather_kernel(sizes, subs, nvar, counts_ref, snaps_ref, basis_ref, stage):
+def gather_kernel(sizes, subs, nvar, counts_ref, snaps_ref, basis_ref, small, stage):
     nx, ny = sizes
     snap_ref, base_ref, proj_ref, square_ref, row_ref, all_ref, snap_sems, base_sems, row_sems = stage
     count, slots, steps = snap_ref.shape
@@ -314,6 +359,9 @@
         return pltpu.make_async_copy(basis_ref.at[i], base_ref.at[i], base_sems.at[i])
 
     for i in range(count):
+        if i == 1:
+            for copy in small:
+                copy.start()
         modes(i).start()
         for c in range(CHUNKS):
             piece(i, c).start()
@@ -331,11 +379,6 @@
         squares = jnp.zeros((SUB, LANES), jnp.float32)
         for c in range(CHUNKS):
             piece(i, c).wait()
-            total = total + jnp.dot(
-                masked[:, c * part : (c + 1) * part],
-                snap_ref[i, c * part : (c + 1) * part, :],
-                preferred_element_type=jnp.float32,
-            )
             for first in range(c * part, (c + 1) * part, ROWS):
                 value = snap_ref[i, first : first + ROWS, :].astype(jnp.float32)
                 value = value * value
@@ -343,10 +386,17 @@
                 node = lax.broadcasted_iota(jnp.int32, (ROWS, LANES), 0) + first
                 value = jnp.where(node < live, value, 0.0)
                 squares = squares + jnp.sum(value.reshape(ROWS // SUB, SUB, LANES), axis=0)
+            total = total + jnp.dot(
+                masked[:, c * part : (c + 1) * part],
+                snap_ref[i, c * part : (c + 1) * part, :],
+                preferred_element_type=jnp.float32,
+            )
         proj_ref[i] = total
         square_ref[i] = squares
         return carry
 
+    for copy in small:
+        copy.wait()
     lax.fori_loop(0, count, project, 0)
 
     pairs = [(v, w) for v in range(nvar) for w in range(v, nvar)]
@@ -453,9 +503,13 @@
         return found
 
 
-def solve_kernel(sizes, subs, nvar, counts_ref, links_ref, snaps_ref, basis_ref, out_ref, state_ref, cell_ref, f_ref, hi_ref, mid_ref, low_ref, halo_sems, *stage):
+def solve_kernel(sizes, subs, nvar, far_counts_ref, far_links_ref, snaps_ref, basis_ref, out_ref, state_ref, counts_ref, links_ref, small_sems, cell_ref, f_ref, hi_ref, mid_ref, low_ref, halo_sems, *stage):
     ranks, steps = state_ref.shape[1:]
-    gnorm, states, sent = gather_kernel(sizes, subs, nvar, counts_ref, snaps_ref, basis_ref, stage)
+    small = [
+        pltpu.make_async_copy(far_counts_ref, counts_ref, small_sems.at[0]),
+        pltpu.make_async_copy(far_links_ref, links_ref, small_sems.at[1]),
+    ]
+    gnorm, states, sent = gather_kernel(sizes, subs, nvar, counts_ref, snaps_ref, basis_ref, small, stage)
     halo = Halo(sizes, subs, cell_ref, halo_sems)
     halo.start(states)
     for s in range(subs):
@@ -490,7 +544,6 @@
     subs, nvar, ranks, slots = basis.shape
     steps = snaps.shape[3]
     wide, nself, nf, full, early, rest, tall = shape_of(subs, ranks, links.shape[1] * ranks)
-    smem = pl.BlockSpec(memory_space=pltpu.SMEM)
     vmem = pl.BlockSpec(memory_space=pltpu.VMEM)
     hbm = pl.BlockSpec(memory_space=pltpu.HBM)
 
@@ -503,9 +556,12 @@
             jax.ShapeDtypeStruct((subs, ranks, nf), jnp.float32),
             jax.ShapeDtypeStruct((subs, ranks, steps), jnp.float32),
         ),
-        in_specs=[smem, smem, hbm, hbm],
+        in_specs=[hbm, hbm, hbm, hbm],
         out_specs=(vmem, vmem),
         scratch_shapes=[
+            pltpu.SMEM(counts.shape, jnp.int32),
+            pltpu.SMEM(links.shape, jnp.int32),
+            pltpu.SemaphoreType.DMA((2,)),
             pltpu.VMEM((3 * (subs + 2), ranks, steps), jnp.float32),
             pltpu.VMEM((subs, tall, steps), jnp.float32),
             pltpu.VMEM((subs, tall, steps), jnp.bfloat16),

time: 40.5 us -> 38.4 us (0.948)
  Pallas kernels: 39.7 us -> 37.6 us
    pallas_call x1, Pallas kernels: 38 us -> 36 us  [solve(): pl.pallas_call(kernel, out_shape=(jax.ShapeDtypeStruct((subs, ranks, nf),...]
where the time goes in v5:
time: 38.4 us; the launch traced here: 38.3 us
  Pallas kernels  37.6 us (98%)
  between operations  0.64 us (2%)
    pallas_call x1, Pallas kernels, solve(): pl.pallas_call(kernel, out_shape=(jax.ShapeDtypeStruct((subs, ranks, nf),...  36 us
    pallas_call x1, Pallas kernels, emit(): pl.pallas_call(emit_kernel, out_shape=(jax.ShapeDtypeStruct(first.shape,...  1.61 us

profile of v5, /device:TPU:0, one launch (start us, length us, event | category | flops | bytes accessed | tf_op | source)
XLA Modules:
  0.0 38.3 jit_solution(11662813576148602614)
XLA Ops:
  0.6 36.0 %solve.1 = (f32[2,24,397]{2,1,0:T(8,128)}, f32[2,24,512]{2,1,0:T(8,128)}) custom-call(s32[2]{0:T(128)} %bitcast.11, s32[2,3]{1,0:T(2,128)} %bitcast.10, bf16[8,2048,512]{2,1,0:T(8,128)(2,1)} %bitcast.8, bf16[8,24,2048]{2,1,0:T(8,128)(2,1)} %bitcast.9), custom_call_target="tpu_custom_call" | custom-call | tf_op jit(solution)/shard_map/solve/pallas_call | solution.py:553
  36.6 1.6 %emit.1 = (f32[2,24,397]{2,1,0:T(8,128)}, f32[2,24,512]{2,1,0:T(8,128)}) custom-call(f32[2,24,397]{2,1,0:T(8,128)} %get-tuple-element.6.first_ref, f32[2,24,512]{2,1,0:T(8,128)} %get-tuple-element.7.second_ref), custom_call_target="tpu_custom_call" | custom-call | tf_op jit(solution)/shard_map/emit/pallas_call | solution.py:598
